TPU v7x, 256 devices: a whole 4x4x8 slice. The times are simulated.
256 devices in a mesh: ep: 32 (over z, x), fsdp: 8 (over y, core).
Axes of the slice: x: 4, y: 4, z: 8, core: 2. Of those that a mesh axis runs over, the one named last changes fastest.
Arguments:
- tokens: bfloat16 [4096, 4096], P('ep', 'fsdp'), may hold values from -6 to 6
- expert_ids: int32 [4096, 2], P('ep'), may hold values from 0 to 7, all different within a row; in each aligned block of 128 rows (0 to 127, 128 to 255, ...) at most 40 rows name the same one
- gate_scores: float32 [4096, 2], P('ep'), may hold values from 0.1 to 1
- gate_weight: bfloat16 [32, 3584, 4096], P('ep', 'fsdp'), may hold values from -0.09375 to 0.09375
- up_weight: bfloat16 [32, 3584, 4096], P('ep', 'fsdp'), may hold values from -0.09375 to 0.09375
- down_weight: bfloat16 [32, 3584, 4096], P('ep', 'fsdp'), may hold values from -0.046875 to 0.046875
Outputs:
- mixed: bfloat16 [4096, 4096], P('ep', 'fsdp')
Inputs may be any that keep to these rules, and one draw needn't show every extreme that they name: `expert_ids`: each row names two different experts. In each aligned block of 128 rows (the rows of one index of ep) no expert is named by more than 40 rows, a bound that some block reaches.
All inputs are finite; a program needn't handle non-finite values.
Results may differ from a plain program's by a relative error of at most 0.014.
Values may be sent and summed in bfloat16 or wider, within the bound.
No kernel may reach another device: no remote copies, remote signals or barrier semaphores. Data moves between devices by JAX's collectives and lax.ppermute only.
A program may use at most 128 MiB of HBM per device.

v0:
```python
import functools

import jax
import jax.numpy as jnp
from jax import lax
from jax.experimental import pallas as pl
from jax.experimental.pallas import tpu as pltpu
from jax.sharding import Mesh, PartitionSpec as P

EXPERTS = 8
CAP = 40
NX = 4
NY = 4
CHUNKS = 2
LANES = 128


PLANE = ("x", "y", "c")


def ring(axis, shift):
    pairs = []
    for x in range(NX):
        for y in range(NY):
            for c in range(2):
                along_x = (c == 0) == (axis == 0)
                tx = (x + shift) % NX if along_x else x
                ty = y if along_x else (y + shift) % NY
                pairs.append(((x * NY + y) * 2 + c, (tx * NY + ty) * 2 + c))
    return pairs


def expert_kernel(where, g0, g1, g2, g3, wg0, wg1, wu0, wu1, wd0, wd1,
                  p0, p1, p2, p3, rows_ref, hid_ref, gate_ref, held_ref, sems):
    core = where[0]
    y = where[1]
    held = (g0, g1, g2, g3)
    outs = (p0, p1, p2, p3)
    blocks = rows_ref.shape[1] // (NY * LANES)
    n, width = g0.shape[1] // blocks, blocks * LANES

    copies = [
        pltpu.make_async_copy(src, held_ref.at[i], sems.at[i])
        for i, src in enumerate((wg0, wu0, wg1, wu1, wd0, wd1))
    ]
    for copy in copies:
        copy.start()

    def columns(k):
        return pl.ds(pl.multiple_of(lax.rem(y - k + NY, NY) * width, width), width)

    def lanes(k, j):
        first = lax.rem(y - k + NY, NY) * width + j * LANES
        return pl.ds(pl.multiple_of(first, LANES), LANES)

    def store(dest, part, r):
        for j in range(blocks):
            dest[j * n:(j + 1) * n] = part[r * n:(r + 1) * n, j * LANES:(j + 1) * LANES]

    for flip in range(2):
        @pl.when(core == flip)
        def _():
            for r in range(4):
                for k in range(4):
                    src = held[k].at[r] if flip == 0 else held[r].at[k]
                    for j in range(blocks):
                        rows_ref[r * n:(r + 1) * n, lanes(k, j)] = src[j * n:(j + 1) * n]

    dims = (((1,), (1,)), ((), ()))

    @pl.loop(0, 4)
    def _(step):
        for i in range(4):
            @pl.when(step == i)
            def _():
                copies[i].wait()
        value = lax.dot_general(
            rows_ref[...], held_ref[step], dims, preferred_element_type=jnp.float32
        )

        @pl.when(lax.rem(step, 2) == 0)
        def _():
            gate_ref[...] = value

        @pl.when(lax.rem(step, 2) == 1)
        def _():
            gate = gate_ref[...]
            hid_ref[lax.div(step, 2)] = (gate / (1.0 + jnp.exp(-gate)) * value).astype(jnp.bfloat16)

    copies[4].wait()
    copies[5].wait()

    @pl.loop(0, 4)
    def _(k):
        part = jnp.dot(hid_ref[0], held_ref[4, :, columns(k)], preferred_element_type=jnp.float32)
        part += jnp.dot(hid_ref[1], held_ref[5, :, columns(k)], preferred_element_type=jnp.float32)
        part = part.astype(jnp.bfloat16)
        for i in range(4):
            @pl.when((core == 0) & (k == i))
            def _():
                for r in range(4):
                    store(outs[i].at[r], part, r)

        @pl.when(core == 1)
        def _():
            for r in range(4):
                store(outs[r].at[k], part, r)


def expert_part(where, held, weights):
    units, dim = weights[0].shape
    n = held[0].shape[1] * held[0].shape[2] * NY // dim
    vmem = pl.BlockSpec(memory_space=pltpu.VMEM)
    return pl.pallas_call(
        expert_kernel,
        out_shape=[jax.ShapeDtypeStruct(held[0].shape, jnp.bfloat16)] * 4,
        in_specs=[pl.BlockSpec(memory_space=pltpu.SMEM)] + [vmem] * 4
        + [pl.BlockSpec(memory_space=pltpu.HBM)] * 6,
        out_specs=[vmem] * 4,
        scratch_shapes=[
            pltpu.VMEM((4 * n, dim), jnp.bfloat16),
            pltpu.VMEM((2, 4 * n, units), jnp.bfloat16),
            pltpu.VMEM((4 * n, units), jnp.float32),
            pltpu.VMEM((6, units, dim), jnp.bfloat16),
            pltpu.SemaphoreType.DMA((6,)),
        ],
        compiler_params=pltpu.CompilerParams(vmem_limit_bytes=48 * 1024 * 1024),
        cost_estimate=pl.CostEstimate(
            flops=2 * 4 * n * dim * units * 6, bytes_accessed=30 << 20, transcendentals=0
        ),
    )(where, *held, *weights)


def dispatch_kernel(ids_ref, tokens_ref, sent_ref, spots_ref):
    tok_rows, feat = tokens_ref.shape
    blocks = feat // LANES
    share = CAP // CHUNKS
    n = share // 2
    unit = blocks * n
    expert = lax.broadcasted_iota(jnp.int32, (EXPERTS, tok_rows), 0)
    named = [ids_ref[k:k + 1] == expert for k in range(2)]
    chosen = (named[0] | named[1]).astype(jnp.float32).astype(jnp.bfloat16)
    before = lax.broadcasted_iota(jnp.int32, (tok_rows, tok_rows), 0)
    before = before < lax.broadcasted_iota(jnp.int32, (tok_rows, tok_rows), 1)
    before = before.astype(jnp.float32).astype(jnp.bfloat16)
    rank = jnp.dot(chosen, before, preferred_element_type=jnp.float32).astype(jnp.int32)
    chunk = (rank >= share).astype(jnp.int32)
    left = rank - chunk * share
    core = (left >= n).astype(jnp.int32)
    group = expert * 2 + core
    row = left - core * n
    spot = group * (CHUNKS * unit) + chunk * unit + row
    at = []
    for k in range(2):
        pick = lambda v: jnp.sum(jnp.where(named[k], v, 0), axis=0, keepdims=True)
        at.append(pick(spot))
        for i in range(CHUNKS):
            held = jnp.where(chunk == i, group * unit + row, -EXPERTS * CAP * blocks)
            spots_ref[k * CHUNKS + i:k * CHUNKS + i + 1] = pick(held)
    at = [jnp.concatenate([a + l * n for l in range(blocks)], axis=1) for a in at]
    sites = sent_ref.shape[0]
    site = lax.broadcasted_iota(jnp.int32, (sites, blocks * tok_rows), 0)
    picker = ((at[0] == site) | (at[1] == site)).astype(jnp.float32).astype(jnp.bfloat16)
    tokens = jnp.concatenate(
        [tokens_ref[:, l * LANES:(l + 1) * LANES] for l in range(blocks)], axis=0
    )
    sent_ref[...] = jnp.dot(picker, tokens, preferred_element_type=jnp.float32).astype(jnp.bfloat16)


def dispatch(ids, tokens):
    tok_rows, feat = tokens.shape
    vmem = pl.BlockSpec(memory_space=pltpu.VMEM)
    return pl.pallas_call(
        dispatch_kernel,
        out_shape=[
            jax.ShapeDtypeStruct((EXPERTS * CAP * feat // LANES, LANES), jnp.bfloat16),
            jax.ShapeDtypeStruct((2 * CHUNKS, tok_rows), jnp.int32),
        ],
        in_specs=[vmem] * 2,
        out_specs=[vmem] * 2,
        compiler_params=pltpu.CompilerParams(vmem_limit_bytes=16 * 1024 * 1024),
    )(ids, tokens)


def combine_kernel(chunk, back_ref, spots_ref, scores_ref, *refs):
    mixed_ref = refs[-1]
    tok_rows, feat = mixed_ref.shape
    n = CAP // CHUNKS // 2
    site = lax.broadcasted_iota(jnp.int32, (tok_rows, back_ref.shape[0]), 1)
    for l in range(feat // LANES):
        cols = slice(l * LANES, (l + 1) * LANES)
        total = refs[0][:, cols] if len(refs) > 1 else 0.0
        for k in range(2):
            i = k * CHUNKS + chunk
            take = spots_ref[:, i:i + 1] + l * n == site
            take = take.astype(jnp.float32).astype(jnp.bfloat16)
            mine = jnp.dot(take, back_ref[...], preferred_element_type=jnp.float32)
            total = total + scores_ref[:, k:k + 1] * mine
        mixed_ref[:, cols] = total.astype(mixed_ref.dtype)


def combine(chunk, back, spots, scores, carried, feat):
    vmem = pl.BlockSpec(memory_space=pltpu.VMEM)
    last = chunk == CHUNKS - 1
    args = (back, spots, scores) + ((carried,) if chunk else ())
    return pl.pallas_call(
        functools.partial(combine_kernel, chunk),
        out_shape=jax.ShapeDtypeStruct(
            (scores.shape[0], feat), jnp.bfloat16 if last else jnp.float32
        ),
        in_specs=[vmem] * len(args),
        out_specs=vmem,
        compiler_params=pltpu.CompilerParams(vmem_limit_bytes=16 * 1024 * 1024),
    )(*args)


def exchange(v):
    return lax.all_to_all(v, ("z", "c"), split_axis=0, concat_axis=0, tiled=True)


def add_up(values):
    total = values[0].astype(jnp.float32)
    for v in values[1:]:
        total = total + v.astype(jnp.float32)
    return total.astype(jnp.bfloat16)


def body(tokens, expert_ids, gate_scores, gate_weight, up_weight, down_weight):
    n_z = lax.axis_size("z")
    _, feat = tokens.shape
    core = lax.axis_index("c")
    where = jnp.stack([core, lax.axis_index("y")]).astype(jnp.int32)

    swap = [(0, 1), (1, 0)]
    weights = []
    for w in (gate_weight[0], up_weight[0], down_weight[0]):
        weights += [w, lax.ppermute(w, "c", swap)]

    n = CAP // CHUNKS // 2
    blocks = feat // LANES
    unit = blocks * n
    sent, spots = dispatch(expert_ids.T, tokens)
    spots = spots.T

    def select(matrix, v, contract):
        return lax.dot_general(
            matrix, v, (((contract,), (0,)), ((), ())), preferred_element_type=jnp.float32
        )

    size = n_z * 2 * unit
    sites = jnp.arange(size, dtype=jnp.int32)
    z_of, rest = lax.div(sites, 2 * unit), lax.rem(sites, 2 * unit)
    moved = lax.div(rest, n) * (n_z * n) + z_of * n + lax.rem(rest, n)
    shuffle = (moved[None, :] == sites[:, None]).astype(jnp.bfloat16)

    got = exchange(sent.reshape(n_z * 2, CHUNKS * unit, LANES))
    got = got.reshape(n_z * 2, CHUNKS, unit, LANES)
    here = jnp.stack([
        select(shuffle, got[:, i].reshape(size, LANES), 1).astype(jnp.bfloat16)
        for i in range(CHUNKS)
    ])

    def permute(v, axis, shift):
        return lax.ppermute(v, PLANE, ring(axis, shift))

    order = (1, 3, 2)
    near = {s: permute(here, 0, s) for s in order}
    held = []
    for i in range(CHUNKS):
        first = jnp.stack([here[i]] + [near[s][i] for s in (1, 2, 3)])
        far = {s: permute(first, 1, s) for s in order}
        held.append((first, far[1], far[2], far[3]))
    parts = [expert_part(where, h, weights) for h in held]

    backs = []
    for part in parts:
        got = [permute(part[s], 1, -s) for s in order]
        total = add_up([part[0]] + got)
        got = [permute(total[s], 0, -s) for s in order]
        back = select(shuffle, add_up([total[0]] + got), 0).astype(jnp.bfloat16)
        back = exchange(back.reshape(n_z * 2, unit, LANES))
        backs.append(back.reshape(size, LANES))

    mixed = None
    for i, back in enumerate(backs):
        mixed = combine(i, back, spots, gate_scores, mixed, feat)
    return mixed


def solution(mesh):
    n_ep = mesh.shape["ep"]
    fine = Mesh(mesh.devices.reshape(n_ep // NX, NX, NY, 2), ("z", "x", "y", "c"))
    ep, fsdp = ("z", "x"), ("y", "c")
    in_specs = (
        P(ep, fsdp),
        P(ep, None),
        P(ep, None),
        P(ep, fsdp, None),
        P(ep, fsdp, None),
        P(ep, fsdp, None),
    )

    return jax.shard_map(body, mesh=fine, in_specs=in_specs, out_specs=P(ep, fsdp), check_vma=False)
```

profile of v0, /device:TPU:2, one launch (start us, length us, event | category | flops | bytes accessed | tf_op | source)
XLA Modules:
  0.0 161.1 jit_solution(3569946181210961242)
XLA Ops:
  3.1 8.6 %all-to-all-start = ((bf16[16,80,128]{2,1,0:T(8,128)(2,1)}), bf16[16,80,128]{2,1,0:T(8,128)(2,1)S(1)}, u32[]{:S(2)}, u32[]{:S(2)}) async-start(bf16[16,80,128]{2,1,0:T(8,128)(2,1)} %bitcast.3), calls=%async_computation | async-start | bytes 655360 | tf_op jit(solution)/shard_map/all_to_all | solution.py:218
  12.6 11.4 %all-to-all-done = bf16[16,80,128]{2,1,0:T(8,128)(2,1)S(1)} async-done(((bf16[16,80,128]{2,1,0:T(8,128)(2,1)}), bf16[16,80,128]{2,1,0:T(8,128)(2,1)S(1)}, u32[]{:S(2)}, u32[]{:S(2)}) %all-to-all-start) | async-done | bytes 327712 | tf_op jit(solution)/shard_map/all_to_all | solution.py:218
  27.6 4.5 %collective-permute-done = bf16[2,640,128]{2,1,0:T(8,128)(2,1)S(1)} collective-permute-done((bf16[2,640,128]{2,1,0:T(8,128)(2,1)S(1)}, bf16[2,640,128]{2,1,0:T(8,128)(2,1)S(1)}, u32[]{:S(2)}, u32[]{:S(2)}) %collective-permute-start) | collective-permute-done | bytes 327712 | tf_op jit(solution)/shard_map/ppermute | solution.py:264
  35.1 4.1 %collective-permute-done.2 = bf16[2,640,128]{2,1,0:T(8,128)(2,1)S(1)} collective-permute-done((bf16[2,640,128]{2,1,0:T(8,128)(2,1)S(1)}, bf16[2,640,128]{2,1,0:T(8,128)(2,1)S(1)}, u32[]{:S(2)}, u32[]{:S(2)}) %collective-permute-start.2) | collective-permute-done | bytes 327712 | tf_op jit(solution)/shard_map/ppermute | solution.py:264
  41.0 2.9 %collective-permute-start.16 = (bf16[4,640,128]{2,1,0:T(8,128)(2,1)S(1)}, bf16[4,640,128]{2,1,0:T(8,128)(2,1)S(1)}, u32[]{:S(2)}, u32[]{:S(2)}) collective-permute-start(bf16[4,640,128]{2,1,0:T(8,128)(2,1)S(1)} %pad_maximum_fusion.1.g0), channel_id=1, source_target_pairs={{0,4},{1,17},{2,6},{3,19},{4,0},{5,21},{6,2},{7,23},{8,12},{9,25},... | collective-permute-start | bytes 1966088 | tf_op jit(solution)/shard_map/ppermute | solution.py:264
  43.9 7.3 %collective-permute-done.15.g1 = bf16[4,640,128]{2,1,0:T(8,128)(2,1)S(1)} collective-permute-done((bf16[4,640,128]{2,1,0:T(8,128)(2,1)S(1)}, bf16[4,640,128]{2,1,0:T(8,128)(2,1)S(1)}, u32[]{:S(2)}, u32[]{:S(2)}) %collective-permute-start.15) | collective-permute-done | bytes 655392 | tf_op jit(solution)/shard_map/ppermute | solution.py:264
  51.2 1.8 %collective-permute-start.17 = (bf16[4,640,128]{2,1,0:T(8,128)(2,1)S(1)}, bf16[4,640,128]{2,1,0:T(8,128)(2,1)S(1)}, u32[]{:S(2)}, u32[]{:S(2)}) collective-permute-start(bf16[4,640,128]{2,1,0:T(8,128)(2,1)S(1)} %pad_maximum_fusion.1.g0), channel_id=1, source_target_pairs={{0,6},{1,25},{2,0},{3,27},{4,2},{5,29},{6,4},{7,31},{8,14},{9,1},{... | collective-permute-start | bytes 1966088 | tf_op jit(solution)/shard_map/ppermute | solution.py:264
  53.1 6.3 %collective-permute-done.16.g2 = bf16[4,640,128]{2,1,0:T(8,128)(2,1)S(1)} collective-permute-done((bf16[4,640,128]{2,1,0:T(8,128)(2,1)S(1)}, bf16[4,640,128]{2,1,0:T(8,128)(2,1)S(1)}, u32[]{:S(2)}, u32[]{:S(2)}) %collective-permute-start.16) | collective-permute-done | bytes 655392 | tf_op jit(solution)/shard_map/ppermute | solution.py:264
  59.4 2.3 %collective-permute-done.17.g3 = bf16[4,640,128]{2,1,0:T(8,128)(2,1)S(1)} collective-permute-done((bf16[4,640,128]{2,1,0:T(8,128)(2,1)S(1)}, bf16[4,640,128]{2,1,0:T(8,128)(2,1)S(1)}, u32[]{:S(2)}, u32[]{:S(2)}) %collective-permute-start.17) | collective-permute-done | bytes 655392 | tf_op jit(solution)/shard_map/ppermute | solution.py:264
  61.8 9.0 %collective-permute-start.4 = (bf16[4,640,128]{2,1,0:T(8,128)(2,1)S(1)}, bf16[4,640,128]{2,1,0:T(8,128)(2,1)S(1)}, u32[]{:S(2)}, u32[]{:S(2)}) collective-permute-start(bf16[4,640,128]{2,1,0:T(8,128)(2,1)S(1)} %pad_maximum_fusion.g0), channel_id=1, source_target_pairs={{0,4},{1,17},{2,6},{3,19},{4,0},{5,21},{6,2},{7,23},{8,12},{9,25},... | collective-permute-start | bytes 1966088 | tf_op jit(solution)/shard_map/ppermute | solution.py:264
  71.4 13.0 %shard_map.66 = (bf16[4,640,128]{2,1,0:T(8,128)(2,1)S(1)}, bf16[4,640,128]{2,1,0:T(8,128)(2,1)S(1)}, bf16[4,640,128]{2,1,0:T(8,128)(2,1)S(1)}, bf16[4,640,128]{2,1,0:T(8,128)(2,1)S(1)}) custom-call(s32[2]{0:T(128)S(1)} %pad_add_fusion.where, bf16[4,640,128]{2,1,0:T(8,128)(2,1)S(1)} %pad_maximum_fusion.1.g0, ...), custom_call_target="tpu_custom_call" | custom-call | flops 7046430720 | bytes 31457280 | tf_op jit(solution)/shard_map/pallas_call | solution.py:114
  84.5 2.0 %collective-permute-start.19 = (bf16[4,640,128]{2,1,0:T(8,128)(2,1)S(1)}, bf16[4,640,128]{2,1,0:T(8,128)(2,1)S(1)}, u32[]{:S(2)}, u32[]{:S(2)}) collective-permute-start(bf16[4,640,128]{2,1,0:T(8,128)(2,1)S(1)} %get-tuple-element.23), channel_id=1, source_target_pairs={{0,2},{1,9},{2,4},{3,11},{4,6},{5,13},{6,0},{7,15},{8,10},{9,17},{... | collective-permute-start | bytes 1966088 | tf_op jit(solution)/shard_map/ppermute | solution.py:264
  88.0 13.0 %shard_map.65 = (bf16[4,640,128]{2,1,0:T(8,128)(2,1)S(1)}, bf16[4,640,128]{2,1,0:T(8,128)(2,1)S(1)}, bf16[4,640,128]{2,1,0:T(8,128)(2,1)S(1)}, bf16[4,640,128]{2,1,0:T(8,128)(2,1)S(1)}) custom-call(s32[2]{0:T(128)S(1)} %pad_add_fusion.where, bf16[4,640,128]{2,1,0:T(8,128)(2,1)S(1)} %pad_maximum_fusion.g0, ...), custom_call_target="tpu_custom_call" | custom-call | flops 7046430720 | bytes 31457280 | tf_op jit(solution)/shard_map/pallas_call | solution.py:114
  101.7 3.4 %collective-permute-start.11 = (bf16[4,640,128]{2,1,0:T(8,128)(2,1)S(1)}, bf16[4,640,128]{2,1,0:T(8,128)(2,1)S(1)}, u32[]{:S(2)}, u32[]{:S(2)}) collective-permute-start(bf16[4,640,128]{2,1,0:T(8,128)(2,1)S(1)} %get-tuple-element.19), channel_id=1, source_target_pairs={{0,4},{1,17},{2,6},{3,19},{4,0},{5,21},{6,2},{7,23},{8,12},{9,25},... | collective-permute-start | bytes 1966088 | tf_op jit(solution)/shard_map/ppermute | solution.py:264
  106.1 1.8 %collective-permute-start.21 = (bf16[640,128]{1,0:T(8,128)(2,1)S(1)}, bf16[640,128]{1,0:T(8,128)(2,1)S(1)}, u32[]{:S(2)}, u32[]{:S(2)}) collective-permute-start(bf16[640,128]{1,0:T(8,128)(2,1)S(1)} %get-tuple-element.25), channel_id=1, source_target_pairs={{0,24},{1,7},{2,26},{3,1},{4,28},{5,3},{6,30},{7,5},{8,0},{9,15},{... | collective-permute-start | bytes 491528 | tf_op jit(solution)/shard_map/ppermute | solution.py:264
  108.2 7.6 %collective-permute-done.10 = bf16[4,640,128]{2,1,0:T(8,128)(2,1)S(1)} collective-permute-done((bf16[4,640,128]{2,1,0:T(8,128)(2,1)S(1)}, bf16[4,640,128]{2,1,0:T(8,128)(2,1)S(1)}, u32[]{:S(2)}, u32[]{:S(2)}) %collective-permute-start.10) | collective-permute-done | bytes 655392 | tf_op jit(solution)/shard_map/ppermute | solution.py:264
  115.8 3.8 %collective-permute-start.23 = (bf16[640,128]{1,0:T(8,128)(2,1)S(1)}, bf16[640,128]{1,0:T(8,128)(2,1)S(1)}, u32[]{:S(2)}, u32[]{:S(2)}) collective-permute-start(bf16[640,128]{1,0:T(8,128)(2,1)S(1)} %get-tuple-element.26), channel_id=1, source_target_pairs={{0,16},{1,5},{2,18},{3,7},{4,20},{5,1},{6,22},{7,3},{8,24},{9,13},... | collective-permute-start | bytes 491528 | tf_op jit(solution)/shard_map/ppermute | solution.py:264
  119.7 4.5 %collective-permute-done.11 = bf16[4,640,128]{2,1,0:T(8,128)(2,1)S(1)} collective-permute-done((bf16[4,640,128]{2,1,0:T(8,128)(2,1)S(1)}, bf16[4,640,128]{2,1,0:T(8,128)(2,1)S(1)}, u32[]{:S(2)}, u32[]{:S(2)}) %collective-permute-start.11) | collective-permute-done | bytes 655392 | tf_op jit(solution)/shard_map/ppermute | solution.py:264
  124.6 1.8 %collective-permute-start.12 = (bf16[640,128]{1,0:T(8,128)(2,1)S(1)}, bf16[640,128]{1,0:T(8,128)(2,1)S(1)}, u32[]{:S(2)}, u32[]{:S(2)}) collective-permute-start(bf16[640,128]{1,0:T(8,128)(2,1)S(1)} %get-tuple-element.28), channel_id=1, source_target_pairs={{0,24},{1,7},{2,26},{3,1},{4,28},{5,3},{6,30},{7,5},{8,0},{9,15},{... | collective-permute-start | bytes 491528 | tf_op jit(solution)/shard_map/ppermute | solution.py:264
  126.7 4.2 %collective-permute-start.14 = (bf16[640,128]{1,0:T(8,128)(2,1)S(1)}, bf16[640,128]{1,0:T(8,128)(2,1)S(1)}, u32[]{:S(2)}, u32[]{:S(2)}) collective-permute-start(bf16[640,128]{1,0:T(8,128)(2,1)S(1)} %get-tuple-element.29), channel_id=1, source_target_pairs={{0,16},{1,5},{2,18},{3,7},{4,20},{5,1},{6,22},{7,3},{8,24},{9,13},... | collective-permute-start | bytes 491528 | tf_op jit(solution)/shard_map/ppermute | solution.py:264
  132.2 5.7 %all-to-all-start.2 = ((bf16[16,40,128]{2,1,0:T(8,128)(2,1)}), bf16[16,40,128]{2,1,0:T(8,128)(2,1)S(1)}, u32[]{:S(2)}, u32[]{:S(2)}) async-start(bf16[16,40,128]{2,1,0:T(8,128)(2,1)} %bitcast.23), calls=%async_computation.2 | async-start | bytes 327680 | tf_op jit(solution)/shard_map/all_to_all | solution.py:218
  139.3 7.9 %all-to-all-done.2 = bf16[16,40,128]{2,1,0:T(8,128)(2,1)S(1)} async-done(((bf16[16,40,128]{2,1,0:T(8,128)(2,1)}), bf16[16,40,128]{2,1,0:T(8,128)(2,1)S(1)}, u32[]{:S(2)}, u32[]{:S(2)}) %all-to-all-start.2) | async-done | bytes 163872 | tf_op jit(solution)/shard_map/all_to_all | solution.py:218
  147.2 3.5 %all-to-all-start.1 = ((bf16[16,40,128]{2,1,0:T(8,128)(2,1)}), bf16[16,40,128]{2,1,0:T(8,128)(2,1)S(1)}, u32[]{:S(2)}, u32[]{:S(2)}) async-start(bf16[16,40,128]{2,1,0:T(8,128)(2,1)} %bitcast.16), calls=%async_computation.1 | async-start | bytes 327680 | tf_op jit(solution)/shard_map/all_to_all | solution.py:218
  151.5 8.4 %all-to-all-done.1 = bf16[16,40,128]{2,1,0:T(8,128)(2,1)S(1)} async-done(((bf16[16,40,128]{2,1,0:T(8,128)(2,1)}), bf16[16,40,128]{2,1,0:T(8,128)(2,1)S(1)}, u32[]{:S(2)}, u32[]{:S(2)}) %all-to-all-start.1) | async-done | bytes 163872 | tf_op jit(solution)/shard_map/all_to_all | solution.py:218
  (60 shorter events, 22.1 us)
Async XLA Ops:
  3.1 21.0 %all-to-all-start = ((bf16[16,80,128]{2,1,0:T(8,128)(2,1)}), bf16[16,80,128]{2,1,0:T(8,128)(2,1)S(1)}, u32[]{:S(2)}, u32[]{:S(2)}) async-start(bf16[16,80,128]{2,1,0:T(8,128)(2,1)} %bitcast.3), calls=%async_computation | async-start | bytes 655360 | tf_op jit(solution)/shard_map/all_to_all | solution.py:218
  11.7 59.1 %collective-permute-start.6 = (bf16[448,4096]{1,0:T(8,128)(2,1)}, bf16[448,4096]{1,0:T(8,128)(2,1)}, u32[]{:S(2)}, u32[]{:S(2)}) collective-permute-start(bf16[448,4096]{1,0:T(8,128)(2,1)} %bitcast.53), channel_id=1, source_target_pairs={{0,1},{1,0},{2,3},{3,2},{4,5},{5,4},{6,7},{7,6},{8,9},{9,8},{10,11... | collective-permute-start | bytes 11010056 | tf_op jit(solution)/shard_map/ppermute | solution.py:237
  12.1 59.3 %collective-permute-start.7 = (bf16[448,4096]{1,0:T(8,128)(2,1)}, bf16[448,4096]{1,0:T(8,128)(2,1)}, u32[]{:S(2)}, u32[]{:S(2)}) collective-permute-start(bf16[448,4096]{1,0:T(8,128)(2,1)} %bitcast.56), channel_id=1, source_target_pairs={{0,1},{1,0},{2,3},{3,2},{4,5},{5,4},{6,7},{7,6},{8,9},{9,8},{10,11... | collective-permute-start | bytes 11010056 | tf_op jit(solution)/shard_map/ppermute | solution.py:237
  12.3 59.1 %collective-permute-start.8 = (bf16[448,4096]{1,0:T(8,128)(2,1)}, bf16[448,4096]{1,0:T(8,128)(2,1)}, u32[]{:S(2)}, u32[]{:S(2)}) collective-permute-start(bf16[448,4096]{1,0:T(8,128)(2,1)} %bitcast.59), channel_id=1, source_target_pairs={{0,1},{1,0},{2,3},{3,2},{4,5},{5,4},{6,7},{7,6},{8,9},{9,8},{10,11... | collective-permute-start | bytes 11010056 | tf_op jit(solution)/shard_map/ppermute | solution.py:237
  39.3 11.9 %collective-permute-start.15 = (bf16[4,640,128]{2,1,0:T(8,128)(2,1)S(1)}, bf16[4,640,128]{2,1,0:T(8,128)(2,1)S(1)}, u32[]{:S(2)}, u32[]{:S(2)}) collective-permute-start(bf16[4,640,128]{2,1,0:T(8,128)(2,1)S(1)} %pad_maximum_fusion.1.g0), channel_id=1, source_target_pairs={{0,2},{1,9},{2,4},{3,11},{4,6},{5,13},{6,0},{7,15},{8,10},{9,17},{... | collective-permute-start | bytes 1966088 | tf_op jit(solution)/shard_map/ppermute | solution.py:264
  41.0 18.5 %collective-permute-start.16 = (bf16[4,640,128]{2,1,0:T(8,128)(2,1)S(1)}, bf16[4,640,128]{2,1,0:T(8,128)(2,1)S(1)}, u32[]{:S(2)}, u32[]{:S(2)}) collective-permute-start(bf16[4,640,128]{2,1,0:T(8,128)(2,1)S(1)} %pad_maximum_fusion.1.g0), channel_id=1, source_target_pairs={{0,4},{1,17},{2,6},{3,19},{4,0},{5,21},{6,2},{7,23},{8,12},{9,25},... | collective-permute-start | bytes 1966088 | tf_op jit(solution)/shard_map/ppermute | solution.py:264
  51.2 10.6 %collective-permute-start.17 = (bf16[4,640,128]{2,1,0:T(8,128)(2,1)S(1)}, bf16[4,640,128]{2,1,0:T(8,128)(2,1)S(1)}, u32[]{:S(2)}, u32[]{:S(2)}) collective-permute-start(bf16[4,640,128]{2,1,0:T(8,128)(2,1)S(1)} %pad_maximum_fusion.1.g0), channel_id=1, source_target_pairs={{0,6},{1,25},{2,0},{3,27},{4,2},{5,29},{6,4},{7,31},{8,14},{9,1},{... | collective-permute-start | bytes 1966088 | tf_op jit(solution)/shard_map/ppermute | solution.py:264
  59.4 27.0 %collective-permute-start.3 = (bf16[4,640,128]{2,1,0:T(8,128)(2,1)S(1)}, bf16[4,640,128]{2,1,0:T(8,128)(2,1)S(1)}, u32[]{:S(2)}, u32[]{:S(2)}) collective-permute-start(bf16[4,640,128]{2,1,0:T(8,128)(2,1)S(1)} %pad_maximum_fusion.g0), channel_id=1, source_target_pairs={{0,2},{1,9},{2,4},{3,11},{4,6},{5,13},{6,0},{7,15},{8,10},{9,17},{... | collective-permute-start | bytes 1966088 | tf_op jit(solution)/shard_map/ppermute | solution.py:264
  61.8 26.2 %collective-permute-start.4 = (bf16[4,640,128]{2,1,0:T(8,128)(2,1)S(1)}, bf16[4,640,128]{2,1,0:T(8,128)(2,1)S(1)}, u32[]{:S(2)}, u32[]{:S(2)}) collective-permute-start(bf16[4,640,128]{2,1,0:T(8,128)(2,1)S(1)} %pad_maximum_fusion.g0), channel_id=1, source_target_pairs={{0,4},{1,17},{2,6},{3,19},{4,0},{5,21},{6,2},{7,23},{8,12},{9,25},... | collective-permute-start | bytes 1966088 | tf_op jit(solution)/shard_map/ppermute | solution.py:264
  70.8 17.2 %collective-permute-start.5 = (bf16[4,640,128]{2,1,0:T(8,128)(2,1)S(1)}, bf16[4,640,128]{2,1,0:T(8,128)(2,1)S(1)}, u32[]{:S(2)}, u32[]{:S(2)}) collective-permute-start(bf16[4,640,128]{2,1,0:T(8,128)(2,1)S(1)} %pad_maximum_fusion.g0), channel_id=1, source_target_pairs={{0,6},{1,25},{2,0},{3,27},{4,2},{5,29},{6,4},{7,31},{8,14},{9,1},{... | collective-permute-start | bytes 1966088 | tf_op jit(solution)/shard_map/ppermute | solution.py:264
  84.4 20.7 %collective-permute-start.18 = (bf16[4,640,128]{2,1,0:T(8,128)(2,1)S(1)}, bf16[4,640,128]{2,1,0:T(8,128)(2,1)S(1)}, u32[]{:S(2)}, u32[]{:S(2)}) collective-permute-start(bf16[4,640,128]{2,1,0:T(8,128)(2,1)S(1)} %get-tuple-element.22), channel_id=1, source_target_pairs={{0,6},{1,25},{2,0},{3,27},{4,2},{5,29},{6,4},{7,31},{8,14},{9,1},{... | collective-permute-start | bytes 1966088 | tf_op jit(solution)/shard_map/ppermute | solution.py:264
  84.5 21.3 %collective-permute-start.19 = (bf16[4,640,128]{2,1,0:T(8,128)(2,1)S(1)}, bf16[4,640,128]{2,1,0:T(8,128)(2,1)S(1)}, u32[]{:S(2)}, u32[]{:S(2)}) collective-permute-start(bf16[4,640,128]{2,1,0:T(8,128)(2,1)S(1)} %get-tuple-element.23), channel_id=1, source_target_pairs={{0,2},{1,9},{2,4},{3,11},{4,6},{5,13},{6,0},{7,15},{8,10},{9,17},{... | collective-permute-start | bytes 1966088 | tf_op jit(solution)/shard_map/ppermute | solution.py:264
  86.5 19.3 %collective-permute-start.20 = (bf16[4,640,128]{2,1,0:T(8,128)(2,1)S(1)}, bf16[4,640,128]{2,1,0:T(8,128)(2,1)S(1)}, u32[]{:S(2)}, u32[]{:S(2)}) collective-permute-start(bf16[4,640,128]{2,1,0:T(8,128)(2,1)S(1)} %get-tuple-element.24), channel_id=1, source_target_pairs={{0,4},{1,17},{2,6},{3,19},{4,0},{5,21},{6,2},{7,23},{8,12},{9,25},... | collective-permute-start | bytes 1966088 | tf_op jit(solution)/shard_map/ppermute | solution.py:264
  101.0 14.9 %collective-permute-start.10 = (bf16[4,640,128]{2,1,0:T(8,128)(2,1)S(1)}, bf16[4,640,128]{2,1,0:T(8,128)(2,1)S(1)}, u32[]{:S(2)}, u32[]{:S(2)}) collective-permute-start(bf16[4,640,128]{2,1,0:T(8,128)(2,1)S(1)} %get-tuple-element.18), channel_id=1, source_target_pairs={{0,2},{1,9},{2,4},{3,11},{4,6},{5,13},{6,0},{7,15},{8,10},{9,17},{... | collective-permute-start | bytes 1966088 | tf_op jit(solution)/shard_map/ppermute | solution.py:264
  101.7 22.5 %collective-permute-start.11 = (bf16[4,640,128]{2,1,0:T(8,128)(2,1)S(1)}, bf16[4,640,128]{2,1,0:T(8,128)(2,1)S(1)}, u32[]{:S(2)}, u32[]{:S(2)}) collective-permute-start(bf16[4,640,128]{2,1,0:T(8,128)(2,1)S(1)} %get-tuple-element.19), channel_id=1, source_target_pairs={{0,4},{1,17},{2,6},{3,19},{4,0},{5,21},{6,2},{7,23},{8,12},{9,25},... | collective-permute-start | bytes 1966088 | tf_op jit(solution)/shard_map/ppermute | solution.py:264
  105.1 19.1 %collective-permute-start.9 = (bf16[4,640,128]{2,1,0:T(8,128)(2,1)S(1)}, bf16[4,640,128]{2,1,0:T(8,128)(2,1)S(1)}, u32[]{:S(2)}, u32[]{:S(2)}) collective-permute-start(bf16[4,640,128]{2,1,0:T(8,128)(2,1)S(1)} %get-tuple-element.17), channel_id=1, source_target_pairs={{0,6},{1,25},{2,0},{3,27},{4,2},{5,29},{6,4},{7,31},{8,14},{9,1},{... | collective-permute-start | bytes 1966088 | tf_op jit(solution)/shard_map/ppermute | solution.py:264
  106.1 20.6 %collective-permute-start.21 = (bf16[640,128]{1,0:T(8,128)(2,1)S(1)}, bf16[640,128]{1,0:T(8,128)(2,1)S(1)}, u32[]{:S(2)}, u32[]{:S(2)}) collective-permute-start(bf16[640,128]{1,0:T(8,128)(2,1)S(1)} %get-tuple-element.25), channel_id=1, source_target_pairs={{0,24},{1,7},{2,26},{3,1},{4,28},{5,3},{6,30},{7,5},{8,0},{9,15},{... | collective-permute-start | bytes 491528 | tf_op jit(solution)/shard_map/ppermute | solution.py:264
  108.0 23.0 %collective-permute-start.22 = (bf16[640,128]{1,0:T(8,128)(2,1)S(1)}, bf16[640,128]{1,0:T(8,128)(2,1)S(1)}, u32[]{:S(2)}, u32[]{:S(2)}) collective-permute-start(bf16[640,128]{1,0:T(8,128)(2,1)S(1)} %get-tuple-element.27), channel_id=1, source_target_pairs={{0,8},{1,3},{2,10},{3,5},{4,12},{5,7},{6,14},{7,1},{8,16},{9,11},{... | collective-permute-start | bytes 491528 | tf_op jit(solution)/shard_map/ppermute | solution.py:264
  115.8 15.1 %collective-permute-start.23 = (bf16[640,128]{1,0:T(8,128)(2,1)S(1)}, bf16[640,128]{1,0:T(8,128)(2,1)S(1)}, u32[]{:S(2)}, u32[]{:S(2)}) collective-permute-start(bf16[640,128]{1,0:T(8,128)(2,1)S(1)} %get-tuple-element.26), channel_id=1, source_target_pairs={{0,16},{1,5},{2,18},{3,7},{4,20},{5,1},{6,22},{7,3},{8,24},{9,13},... | collective-permute-start | bytes 491528 | tf_op jit(solution)/shard_map/ppermute | solution.py:264
  124.6 13.4 %collective-permute-start.12 = (bf16[640,128]{1,0:T(8,128)(2,1)S(1)}, bf16[640,128]{1,0:T(8,128)(2,1)S(1)}, u32[]{:S(2)}, u32[]{:S(2)}) collective-permute-start(bf16[640,128]{1,0:T(8,128)(2,1)S(1)} %get-tuple-element.28), channel_id=1, source_target_pairs={{0,24},{1,7},{2,26},{3,1},{4,28},{5,3},{6,30},{7,5},{8,0},{9,15},{... | collective-permute-start | bytes 491528 | tf_op jit(solution)/shard_map/ppermute | solution.py:264
  126.4 11.6 %collective-permute-start.13 = (bf16[640,128]{1,0:T(8,128)(2,1)S(1)}, bf16[640,128]{1,0:T(8,128)(2,1)S(1)}, u32[]{:S(2)}, u32[]{:S(2)}) collective-permute-start(bf16[640,128]{1,0:T(8,128)(2,1)S(1)} %get-tuple-element.30), channel_id=1, source_target_pairs={{0,8},{1,3},{2,10},{3,5},{4,12},{5,7},{6,14},{7,1},{8,16},{9,11},{... | collective-permute-start | bytes 491528 | tf_op jit(solution)/shard_map/ppermute | solution.py:264
  126.7 11.3 %collective-permute-start.14 = (bf16[640,128]{1,0:T(8,128)(2,1)S(1)}, bf16[640,128]{1,0:T(8,128)(2,1)S(1)}, u32[]{:S(2)}, u32[]{:S(2)}) collective-permute-start(bf16[640,128]{1,0:T(8,128)(2,1)S(1)} %get-tuple-element.29), channel_id=1, source_target_pairs={{0,16},{1,5},{2,18},{3,7},{4,20},{5,1},{6,22},{7,3},{8,24},{9,13},... | collective-permute-start | bytes 491528 | tf_op jit(solution)/shard_map/ppermute | solution.py:264
  132.2 14.9 %all-to-all-start.2 = ((bf16[16,40,128]{2,1,0:T(8,128)(2,1)}), bf16[16,40,128]{2,1,0:T(8,128)(2,1)S(1)}, u32[]{:S(2)}, u32[]{:S(2)}) async-start(bf16[16,40,128]{2,1,0:T(8,128)(2,1)} %bitcast.23), calls=%async_computation.2 | async-start | bytes 327680 | tf_op jit(solution)/shard_map/all_to_all | solution.py:218
  147.2 12.7 %all-to-all-start.1 = ((bf16[16,40,128]{2,1,0:T(8,128)(2,1)}), bf16[16,40,128]{2,1,0:T(8,128)(2,1)S(1)}, u32[]{:S(2)}, u32[]{:S(2)}) async-start(bf16[16,40,128]{2,1,0:T(8,128)(2,1)} %bitcast.16), calls=%async_computation.1 | async-start | bytes 327680 | tf_op jit(solution)/shard_map/all_to_all | solution.py:218
  (6 other events, 48.5 us)
where the time goes:
time: 162 us; the launch traced here: 161 us
  waiting for transfers between devices  65.6 us (40%)
  starting transfers between devices  59.7 us (37%)
  Pallas kernels  29.3 us (18%)
  matrix products  3.42 us (2%)
  local copies, waits for them, and re-layouts  1.98 us (1%)
    ppermute x21, starting transfers between devices, permute(): return lax.ppermute(v, PLANE, ring(axis, shift))  41 us
    ppermute x21, waiting for transfers between devices, permute(): return lax.ppermute(v, PLANE, ring(axis, shift))  37.9 us
    all_to_all x3, waiting for transfers between devices, exchange(): lax.all_to_all(v, ('z', 'c'), split_axis=0, concat_axis=0, tiled=True)  27.7 us
    pallas_call x2, Pallas kernels, expert_part(): pl.pallas_call(expert_kernel, out_shape=[jax.ShapeDtypeStruct(held[0].sha...  26 us
    all_to_all x3, starting transfers between devices, exchange(): lax.all_to_all(v, ('z', 'c'), split_axis=0, concat_axis=0, tiled=True)  17.8 us
    dot_general x4, matrix products, select(): lax.dot_general(matrix, v, (((contract,), (0,)), ((), ())), preferred_ele...  3.42 us
  transfers between devices with their start and end apart: 27, of which 11 were waited for; matrix products, arithmetic and copies ran while one was open for 3% of the time, Pallas kernels for 16%

commit v1 on v0

--- a/solution.py
+++ b/solution.py
@@ -1,5 +1,3 @@
-import functools
-
 import jax
 import jax.numpy as jnp
 from jax import lax
@@ -43,7 +41,7 @@
         pltpu.make_async_copy(src, held_ref.at[i], sems.at[i])
         for i, src in enumerate((wg0, wu0, wg1, wu1, wd0, wd1))
     ]
-    for copy in copies:
+    for copy in copies[:2]:
         copy.start()
 
     def columns(k):
@@ -74,6 +72,7 @@
             @pl.when(step == i)
             def _():
                 copies[i].wait()
+                copies[i + 2].start()
         value = lax.dot_general(
             rows_ref[...], held_ref[step], dims, preferred_element_type=jnp.float32
         )
@@ -152,11 +151,8 @@
     spot = group * (CHUNKS * unit) + chunk * unit + row
     at = []
     for k in range(2):
-        pick = lambda v: jnp.sum(jnp.where(named[k], v, 0), axis=0, keepdims=True)
-        at.append(pick(spot))
-        for i in range(CHUNKS):
-            held = jnp.where(chunk == i, group * unit + row, -EXPERTS * CAP * blocks)
-            spots_ref[k * CHUNKS + i:k * CHUNKS + i + 1] = pick(held)
+        at.append(jnp.sum(jnp.where(named[k], spot, 0), axis=0, keepdims=True))
+        spots_ref[k:k + 1] = at[k]
     at = [jnp.concatenate([a + l * n for l in range(blocks)], axis=1) for a in at]
     sites = sent_ref.shape[0]
     site = lax.broadcasted_iota(jnp.int32, (sites, blocks * tok_rows), 0)
@@ -174,7 +170,7 @@
         dispatch_kernel,
         out_shape=[
             jax.ShapeDtypeStruct((EXPERTS * CAP * feat // LANES, LANES), jnp.bfloat16),
-            jax.ShapeDtypeStruct((2 * CHUNKS, tok_rows), jnp.int32),
+            jax.ShapeDtypeStruct((2, tok_rows), jnp.int32),
         ],
         in_specs=[vmem] * 2,
         out_specs=[vmem] * 2,
@@ -182,32 +178,36 @@
     )(ids, tokens)
 
 
-def combine_kernel(chunk, back_ref, spots_ref, scores_ref, *refs):
-    mixed_ref = refs[-1]
-    tok_rows, feat = mixed_ref.shape
+def plan_kernel(spots_ref, take_ref):
     n = CAP // CHUNKS // 2
-    site = lax.broadcasted_iota(jnp.int32, (tok_rows, back_ref.shape[0]), 1)
-    for l in range(feat // LANES):
-        cols = slice(l * LANES, (l + 1) * LANES)
-        total = refs[0][:, cols] if len(refs) > 1 else 0.0
+    tok_rows = spots_ref.shape[0]
+    site = lax.broadcasted_iota(jnp.int32, (tok_rows, take_ref.shape[2]), 1)
+    for k in range(take_ref.shape[0]):
+        for l in range(take_ref.shape[1] // tok_rows):
+            take = spots_ref[:, k:k + 1] + l * n == site
+            take_ref[k, l * tok_rows:(l + 1) * tok_rows] = (
+                take.astype(jnp.float32).astype(jnp.bfloat16)
+            )
+
+
+def combine_kernel(back_ref, take_ref, scores_ref, mixed_ref):
+    tok_rows = mixed_ref.shape[0]
+    for l in range(mixed_ref.shape[1] // LANES):
+        total = jnp.zeros((tok_rows, LANES), jnp.float32)
         for k in range(2):
-            i = k * CHUNKS + chunk
-            take = spots_ref[:, i:i + 1] + l * n == site
-            take = take.astype(jnp.float32).astype(jnp.bfloat16)
-            mine = jnp.dot(take, back_ref[...], preferred_element_type=jnp.float32)
+            mine = jnp.dot(
+                take_ref[k, l * tok_rows:(l + 1) * tok_rows], back_ref[...],
+                preferred_element_type=jnp.float32,
+            )
             total = total + scores_ref[:, k:k + 1] * mine
-        mixed_ref[:, cols] = total.astype(mixed_ref.dtype)
-
-
-def combine(chunk, back, spots, scores, carried, feat):
+        mixed_ref[:, l * LANES:(l + 1) * LANES] = total.astype(mixed_ref.dtype)
+
+
+def local_call(kernel, out, *args):
     vmem = pl.BlockSpec(memory_space=pltpu.VMEM)
-    last = chunk == CHUNKS - 1
-    args = (back, spots, scores) + ((carried,) if chunk else ())
     return pl.pallas_call(
-        functools.partial(combine_kernel, chunk),
-        out_shape=jax.ShapeDtypeStruct(
-            (scores.shape[0], feat), jnp.bfloat16 if last else jnp.float32
-        ),
+        kernel,
+        out_shape=out,
         in_specs=[vmem] * len(args),
         out_specs=vmem,
         compiler_params=pltpu.CompilerParams(vmem_limit_bytes=16 * 1024 * 1024),
@@ -227,7 +227,7 @@
 
 def body(tokens, expert_ids, gate_scores, gate_weight, up_weight, down_weight):
     n_z = lax.axis_size("z")
-    _, feat = tokens.shape
+    tok_rows, feat = tokens.shape
     core = lax.axis_index("c")
     where = jnp.stack([core, lax.axis_index("y")]).astype(jnp.int32)
 
@@ -278,13 +278,18 @@
         total = add_up([part[0]] + got)
         got = [permute(total[s], 0, -s) for s in order]
         back = select(shuffle, add_up([total[0]] + got), 0).astype(jnp.bfloat16)
-        back = exchange(back.reshape(n_z * 2, unit, LANES))
-        backs.append(back.reshape(size, LANES))
-
-    mixed = None
-    for i, back in enumerate(backs):
-        mixed = combine(i, back, spots, gate_scores, mixed, feat)
-    return mixed
+        backs.append(back.reshape(n_z * 2, unit, LANES))
+
+    back = exchange(jnp.concatenate(backs, axis=1)).reshape(CHUNKS * size, LANES)
+    tok_rows = tokens.shape[0]
+    take = local_call(
+        plan_kernel,
+        jax.ShapeDtypeStruct((2, blocks * tok_rows, CHUNKS * size), jnp.bfloat16),
+        spots,
+    )
+    return local_call(
+        combine_kernel, jax.ShapeDtypeStruct(tokens.shape, tokens.dtype), back, take, gate_scores
+    )
 
 
 def solution(mesh):

time: 162 us -> 161 us (level)
  the two profiles are of different devices: /device:TPU:2 before, /device:TPU:1 now
where the time goes in v1:
time: 161 us; the launch traced here: 160 us
  starting transfers between devices  71.8 us (45%)
  waiting for transfers between devices  52.1 us (32%)
  Pallas kernels  30.3 us (19%)
  matrix products  2.08 us (1%)
  local copies, waits for them, and re-layouts  1.97 us (1%)
  other arithmetic  1.74 us (1%)
    ppermute x21, starting transfers between devices, permute(): return lax.ppermute(v, PLANE, ring(axis, shift))  50.5 us
    ppermute x21, waiting for transfers between devices, permute(): return lax.ppermute(v, PLANE, ring(axis, shift))  27.3 us
    pallas_call x2, Pallas kernels, expert_part(): pl.pallas_call(expert_kernel, out_shape=[jax.ShapeDtypeStruct(held[0].sha...  26.8 us
    all_to_all x2, waiting for transfers between devices, exchange(): lax.all_to_all(v, ('z', 'c'), split_axis=0, concat_axis=0, tiled=True)  24.8 us
    all_to_all x2, starting transfers between devices, exchange(): lax.all_to_all(v, ('z', 'c'), split_axis=0, concat_axis=0, tiled=True)  20.6 us
  transfers between devices with their start and end apart: 26, of which 10 were waited for; matrix products, arithmetic and copies ran while one was open for 2% of the time, Pallas kernels for 17%

profile of v1, /device:TPU:1, one launch (start us, length us, event | category | flops | bytes accessed | tf_op | source)
XLA Modules:
  0.0 160.2 jit_solution(11231630987786177534)
XLA Ops:
  1.6 1.5 shard_map.64
  3.1 10.0 %all-to-all-start = ((bf16[16,80,128]{2,1,0:T(8,128)(2,1)}), bf16[16,80,128]{2,1,0:T(8,128)(2,1)S(1)}, u32[]{:S(2)}, u32[]{:S(2)}) async-start(bf16[16,80,128]{2,1,0:T(8,128)(2,1)} %bitcast.3), calls=%async_computation | async-start | bytes 655360 | tf_op jit(solution)/shard_map/all_to_all | solution.py:218
  13.8 12.3 %all-to-all-done = bf16[16,80,128]{2,1,0:T(8,128)(2,1)S(1)} async-done(((bf16[16,80,128]{2,1,0:T(8,128)(2,1)}), bf16[16,80,128]{2,1,0:T(8,128)(2,1)S(1)}, u32[]{:S(2)}, u32[]{:S(2)}) %all-to-all-start) | async-done | bytes 327712 | tf_op jit(solution)/shard_map/all_to_all | solution.py:218
  28.3 2.6 %collective-permute-start.1 = (bf16[2,640,128]{2,1,0:T(8,128)(2,1)S(1)}, bf16[2,640,128]{2,1,0:T(8,128)(2,1)S(1)}, u32[]{:S(2)}, u32[]{:S(2)}) collective-permute-start(bf16[2,640,128]{2,1,0:T(8,128)(2,1)S(1)} %pad_maximum_fusion.2), channel_id=1, source_target_pairs={{0,16},{1,5},{2,18},{3,7},{4,20},{5,1},{6,22},{7,3},{8,24},{9,13},... | collective-permute-start | bytes 983048 | tf_op jit(solution)/shard_map/ppermute | solution.py:264
  30.9 3.5 %collective-permute-done = bf16[2,640,128]{2,1,0:T(8,128)(2,1)S(1)} collective-permute-done((bf16[2,640,128]{2,1,0:T(8,128)(2,1)S(1)}, bf16[2,640,128]{2,1,0:T(8,128)(2,1)S(1)}, u32[]{:S(2)}, u32[]{:S(2)}) %collective-permute-start) | collective-permute-done | bytes 327712 | tf_op jit(solution)/shard_map/ppermute | solution.py:264
  34.4 1.6 collective-permute-start.2
  36.0 2.9 %collective-permute-done.1 = bf16[2,640,128]{2,1,0:T(8,128)(2,1)S(1)} collective-permute-done((bf16[2,640,128]{2,1,0:T(8,128)(2,1)S(1)}, bf16[2,640,128]{2,1,0:T(8,128)(2,1)S(1)}, u32[]{:S(2)}, u32[]{:S(2)}) %collective-permute-start.1) | collective-permute-done | bytes 327712 | tf_op jit(solution)/shard_map/ppermute | solution.py:264
  39.0 1.7 %collective-permute-done.2 = bf16[2,640,128]{2,1,0:T(8,128)(2,1)S(1)} collective-permute-done((bf16[2,640,128]{2,1,0:T(8,128)(2,1)S(1)}, bf16[2,640,128]{2,1,0:T(8,128)(2,1)S(1)}, u32[]{:S(2)}, u32[]{:S(2)}) %collective-permute-start.2) | collective-permute-done | bytes 327712 | tf_op jit(solution)/shard_map/ppermute | solution.py:264
  41.7 2.9 %collective-permute-start.4 = (bf16[4,640,128]{2,1,0:T(8,128)(2,1)S(1)}, bf16[4,640,128]{2,1,0:T(8,128)(2,1)S(1)}, u32[]{:S(2)}, u32[]{:S(2)}) collective-permute-start(bf16[4,640,128]{2,1,0:T(8,128)(2,1)S(1)} %pad_maximum_fusion.g0), channel_id=1, source_target_pairs={{0,4},{1,17},{2,6},{3,19},{4,0},{5,21},{6,2},{7,23},{8,12},{9,25},... | collective-permute-start | bytes 1966088 | tf_op jit(solution)/shard_map/ppermute | solution.py:264
  44.6 7.2 %collective-permute-done.3.g1 = bf16[4,640,128]{2,1,0:T(8,128)(2,1)S(1)} collective-permute-done((bf16[4,640,128]{2,1,0:T(8,128)(2,1)S(1)}, bf16[4,640,128]{2,1,0:T(8,128)(2,1)S(1)}, u32[]{:S(2)}, u32[]{:S(2)}) %collective-permute-start.3) | collective-permute-done | bytes 655392 | tf_op jit(solution)/shard_map/ppermute | solution.py:264
  53.3 6.6 %collective-permute-done.4.g2 = bf16[4,640,128]{2,1,0:T(8,128)(2,1)S(1)} collective-permute-done((bf16[4,640,128]{2,1,0:T(8,128)(2,1)S(1)}, bf16[4,640,128]{2,1,0:T(8,128)(2,1)S(1)}, u32[]{:S(2)}, u32[]{:S(2)}) %collective-permute-start.4) | collective-permute-done | bytes 655392 | tf_op jit(solution)/shard_map/ppermute | solution.py:264
  59.9 1.6 %collective-permute-done.5.g3 = bf16[4,640,128]{2,1,0:T(8,128)(2,1)S(1)} collective-permute-done((bf16[4,640,128]{2,1,0:T(8,128)(2,1)S(1)}, bf16[4,640,128]{2,1,0:T(8,128)(2,1)S(1)}, u32[]{:S(2)}, u32[]{:S(2)}) %collective-permute-start.5) | collective-permute-done | bytes 655392 | tf_op jit(solution)/shard_map/ppermute | solution.py:264
  64.1 13.4 %shard_map.65 = (bf16[4,640,128]{2,1,0:T(8,128)(2,1)S(1)}, bf16[4,640,128]{2,1,0:T(8,128)(2,1)S(1)}, bf16[4,640,128]{2,1,0:T(8,128)(2,1)S(1)}, bf16[4,640,128]{2,1,0:T(8,128)(2,1)S(1)}) custom-call(s32[2]{0:T(128)S(1)} %pad_add_fusion.where, bf16[4,640,128]{2,1,0:T(8,128)(2,1)S(1)} %pad_maximum_fusion.g0, ...), custom_call_target="tpu_custom_call" | custom-call | flops 7046430720 | bytes 31457280 | tf_op jit(solution)/shard_map/pallas_call | solution.py:113
  78.2 1.9 %collective-permute-start.11 = (bf16[4,640,128]{2,1,0:T(8,128)(2,1)S(1)}, bf16[4,640,128]{2,1,0:T(8,128)(2,1)S(1)}, u32[]{:S(2)}, u32[]{:S(2)}) collective-permute-start(bf16[4,640,128]{2,1,0:T(8,128)(2,1)S(1)} %get-tuple-element.19), channel_id=1, source_target_pairs={{0,4},{1,17},{2,6},{3,19},{4,0},{5,21},{6,2},{7,23},{8,12},{9,25},... | collective-permute-start | bytes 1966088 | tf_op jit(solution)/shard_map/ppermute | solution.py:264
  80.0 2.0 %collective-permute-start.9 = (bf16[4,640,128]{2,1,0:T(8,128)(2,1)S(1)}, bf16[4,640,128]{2,1,0:T(8,128)(2,1)S(1)}, u32[]{:S(2)}, u32[]{:S(2)}) collective-permute-start(bf16[4,640,128]{2,1,0:T(8,128)(2,1)S(1)} %get-tuple-element.17), channel_id=1, source_target_pairs={{0,6},{1,25},{2,0},{3,27},{4,2},{5,29},{6,4},{7,31},{8,14},{9,1},{... | collective-permute-start | bytes 1966088 | tf_op jit(solution)/shard_map/ppermute | solution.py:264
  82.0 13.4 %shard_map.66 = (bf16[4,640,128]{2,1,0:T(8,128)(2,1)S(1)}, bf16[4,640,128]{2,1,0:T(8,128)(2,1)S(1)}, bf16[4,640,128]{2,1,0:T(8,128)(2,1)S(1)}, bf16[4,640,128]{2,1,0:T(8,128)(2,1)S(1)}) custom-call(s32[2]{0:T(128)S(1)} %pad_add_fusion.where, bf16[4,640,128]{2,1,0:T(8,128)(2,1)S(1)} %pad_maximum_fusion.1.g0, ...), custom_call_target="tpu_custom_call" | custom-call | flops 7046430720 | bytes 31457280 | tf_op jit(solution)/shard_map/pallas_call | solution.py:113
  98.0 9.9 %collective-permute-start.12 = (bf16[640,128]{1,0:T(8,128)(2,1)S(1)}, bf16[640,128]{1,0:T(8,128)(2,1)S(1)}, u32[]{:S(2)}, u32[]{:S(2)}) collective-permute-start(bf16[640,128]{1,0:T(8,128)(2,1)S(1)} %get-tuple-element.25), channel_id=1, source_target_pairs={{0,24},{1,7},{2,26},{3,1},{4,28},{5,3},{6,30},{7,5},{8,0},{9,15},{... | collective-permute-start | bytes 491528 | tf_op jit(solution)/shard_map/ppermute | solution.py:264
  107.9 8.3 %collective-permute-start.14 = (bf16[640,128]{1,0:T(8,128)(2,1)S(1)}, bf16[640,128]{1,0:T(8,128)(2,1)S(1)}, u32[]{:S(2)}, u32[]{:S(2)}) collective-permute-start(bf16[640,128]{1,0:T(8,128)(2,1)S(1)} %get-tuple-element.26), channel_id=1, source_target_pairs={{0,16},{1,5},{2,18},{3,7},{4,20},{5,1},{6,22},{7,3},{8,24},{9,13},... | collective-permute-start | bytes 491528 | tf_op jit(solution)/shard_map/ppermute | solution.py:264
  116.6 8.3 %collective-permute-start.21 = (bf16[640,128]{1,0:T(8,128)(2,1)S(1)}, bf16[640,128]{1,0:T(8,128)(2,1)S(1)}, u32[]{:S(2)}, u32[]{:S(2)}) collective-permute-start(bf16[640,128]{1,0:T(8,128)(2,1)S(1)} %get-tuple-element.28), channel_id=1, source_target_pairs={{0,24},{1,7},{2,26},{3,1},{4,28},{5,3},{6,30},{7,5},{8,0},{9,15},{... | collective-permute-start | bytes 491528 | tf_op jit(solution)/shard_map/ppermute | solution.py:264
  126.1 2.8 %collective-permute-start.23 = (bf16[640,128]{1,0:T(8,128)(2,1)S(1)}, bf16[640,128]{1,0:T(8,128)(2,1)S(1)}, u32[]{:S(2)}, u32[]{:S(2)}) collective-permute-start(bf16[640,128]{1,0:T(8,128)(2,1)S(1)} %get-tuple-element.29), channel_id=1, source_target_pairs={{0,16},{1,5},{2,18},{3,7},{4,20},{5,1},{6,22},{7,3},{8,24},{9,13},... | collective-permute-start | bytes 491528 | tf_op jit(solution)/shard_map/ppermute | solution.py:264
  130.4 2.9 %collective-permute-done.23 = bf16[640,128]{1,0:T(8,128)(2,1)S(1)} collective-permute-done((bf16[640,128]{1,0:T(8,128)(2,1)S(1)}, bf16[640,128]{1,0:T(8,128)(2,1)S(1)}, u32[]{:S(2)}, u32[]{:S(2)}) %collective-permute-start.23) | collective-permute-done | bytes 163872 | tf_op jit(solution)/shard_map/ppermute | solution.py:264
  134.8 10.7 %all-to-all-start.1 = ((bf16[16,80,128]{2,1,0:T(8,128)(2,1)}), bf16[16,80,128]{2,1,0:T(8,128)(2,1)S(1)}, u32[]{:S(2)}, u32[]{:S(2)}) async-start(bf16[16,80,128]{2,1,0:T(8,128)(2,1)} %pad_maximum_fusion.3), calls=%async_computation.1 | async-start | bytes 655360 | tf_op jit(solution)/shard_map/all_to_all | solution.py:218
  146.2 12.5 %all-to-all-done.1 = bf16[16,80,128]{2,1,0:T(8,128)(2,1)S(1)} async-done(((bf16[16,80,128]{2,1,0:T(8,128)(2,1)}), bf16[16,80,128]{2,1,0:T(8,128)(2,1)S(1)}, u32[]{:S(2)}, u32[]{:S(2)}) %all-to-all-start.1) | async-done | bytes 327712 | tf_op jit(solution)/shard_map/all_to_all | solution.py:218
  158.7 1.5 shard_map.68
  (59 shorter events, 18.1 us)
Async XLA Ops:
  3.1 22.9 %all-to-all-start = ((bf16[16,80,128]{2,1,0:T(8,128)(2,1)}), bf16[16,80,128]{2,1,0:T(8,128)(2,1)S(1)}, u32[]{:S(2)}, u32[]{:S(2)}) async-start(bf16[16,80,128]{2,1,0:T(8,128)(2,1)} %bitcast.3), calls=%async_computation | async-start | bytes 655360 | tf_op jit(solution)/shard_map/all_to_all | solution.py:218
  13.1 49.6 %collective-permute-start.6 = (bf16[448,4096]{1,0:T(8,128)(2,1)}, bf16[448,4096]{1,0:T(8,128)(2,1)}, u32[]{:S(2)}, u32[]{:S(2)}) collective-permute-start(bf16[448,4096]{1,0:T(8,128)(2,1)} %bitcast.52), channel_id=1, source_target_pairs={{0,1},{1,0},{2,3},{3,2},{4,5},{5,4},{6,7},{7,6},{8,9},{9,8},{10,11... | collective-permute-start | bytes 11010056 | tf_op jit(solution)/shard_map/ppermute | solution.py:237
  13.3 50.8 %collective-permute-start.7 = (bf16[448,4096]{1,0:T(8,128)(2,1)}, bf16[448,4096]{1,0:T(8,128)(2,1)}, u32[]{:S(2)}, u32[]{:S(2)}) collective-permute-start(bf16[448,4096]{1,0:T(8,128)(2,1)} %bitcast.55), channel_id=1, source_target_pairs={{0,1},{1,0},{2,3},{3,2},{4,5},{5,4},{6,7},{7,6},{8,9},{9,8},{10,11... | collective-permute-start | bytes 11010056 | tf_op jit(solution)/shard_map/ppermute | solution.py:237
  13.6 50.5 %collective-permute-start.8 = (bf16[448,4096]{1,0:T(8,128)(2,1)}, bf16[448,4096]{1,0:T(8,128)(2,1)}, u32[]{:S(2)}, u32[]{:S(2)}) collective-permute-start(bf16[448,4096]{1,0:T(8,128)(2,1)} %bitcast.58), channel_id=1, source_target_pairs={{0,1},{1,0},{2,3},{3,2},{4,5},{5,4},{6,7},{7,6},{8,9},{9,8},{10,11... | collective-permute-start | bytes 11010056 | tf_op jit(solution)/shard_map/ppermute | solution.py:237
  26.9 7.5 %collective-permute-start = (bf16[2,640,128]{2,1,0:T(8,128)(2,1)S(1)}, bf16[2,640,128]{2,1,0:T(8,128)(2,1)S(1)}, u32[]{:S(2)}, u32[]{:S(2)}) collective-permute-start(bf16[2,640,128]{2,1,0:T(8,128)(2,1)S(1)} %pad_maximum_fusion.2), channel_id=1, source_target_pairs={{0,8},{1,3},{2,10},{3,5},{4,12},{5,7},{6,14},{7,1},{8,16},{9,11},{... | collective-permute-start | bytes 983048 | tf_op jit(solution)/shard_map/ppermute | solution.py:264
  28.3 10.6 %collective-permute-start.1 = (bf16[2,640,128]{2,1,0:T(8,128)(2,1)S(1)}, bf16[2,640,128]{2,1,0:T(8,128)(2,1)S(1)}, u32[]{:S(2)}, u32[]{:S(2)}) collective-permute-start(bf16[2,640,128]{2,1,0:T(8,128)(2,1)S(1)} %pad_maximum_fusion.2), channel_id=1, source_target_pairs={{0,16},{1,5},{2,18},{3,7},{4,20},{5,1},{6,22},{7,3},{8,24},{9,13},... | collective-permute-start | bytes 983048 | tf_op jit(solution)/shard_map/ppermute | solution.py:264
  40.8 11.0 %collective-permute-start.3 = (bf16[4,640,128]{2,1,0:T(8,128)(2,1)S(1)}, bf16[4,640,128]{2,1,0:T(8,128)(2,1)S(1)}, u32[]{:S(2)}, u32[]{:S(2)}) collective-permute-start(bf16[4,640,128]{2,1,0:T(8,128)(2,1)S(1)} %pad_maximum_fusion.g0), channel_id=1, source_target_pairs={{0,2},{1,9},{2,4},{3,11},{4,6},{5,13},{6,0},{7,15},{8,10},{9,17},{... | collective-permute-start | bytes 1966088 | tf_op jit(solution)/shard_map/ppermute | solution.py:264
  41.7 18.2 %collective-permute-start.4 = (bf16[4,640,128]{2,1,0:T(8,128)(2,1)S(1)}, bf16[4,640,128]{2,1,0:T(8,128)(2,1)S(1)}, u32[]{:S(2)}, u32[]{:S(2)}) collective-permute-start(bf16[4,640,128]{2,1,0:T(8,128)(2,1)S(1)} %pad_maximum_fusion.g0), channel_id=1, source_target_pairs={{0,4},{1,17},{2,6},{3,19},{4,0},{5,21},{6,2},{7,23},{8,12},{9,25},... | collective-permute-start | bytes 1966088 | tf_op jit(solution)/shard_map/ppermute | solution.py:264
  51.8 9.7 %collective-permute-start.5 = (bf16[4,640,128]{2,1,0:T(8,128)(2,1)S(1)}, bf16[4,640,128]{2,1,0:T(8,128)(2,1)S(1)}, u32[]{:S(2)}, u32[]{:S(2)}) collective-permute-start(bf16[4,640,128]{2,1,0:T(8,128)(2,1)S(1)} %pad_maximum_fusion.g0), channel_id=1, source_target_pairs={{0,6},{1,25},{2,0},{3,27},{4,2},{5,29},{6,4},{7,31},{8,14},{9,1},{... | collective-permute-start | bytes 1966088 | tf_op jit(solution)/shard_map/ppermute | solution.py:264
  59.9 20.2 %collective-permute-start.15 = (bf16[4,640,128]{2,1,0:T(8,128)(2,1)S(1)}, bf16[4,640,128]{2,1,0:T(8,128)(2,1)S(1)}, u32[]{:S(2)}, u32[]{:S(2)}) collective-permute-start(bf16[4,640,128]{2,1,0:T(8,128)(2,1)S(1)} %pad_maximum_fusion.1.g0), channel_id=1, source_target_pairs={{0,2},{1,9},{2,4},{3,11},{4,6},{5,13},{6,0},{7,15},{8,10},{9,17},{... | collective-permute-start | bytes 1966088 | tf_op jit(solution)/shard_map/ppermute | solution.py:264
  61.5 20.5 %collective-permute-start.16 = (bf16[4,640,128]{2,1,0:T(8,128)(2,1)S(1)}, bf16[4,640,128]{2,1,0:T(8,128)(2,1)S(1)}, u32[]{:S(2)}, u32[]{:S(2)}) collective-permute-start(bf16[4,640,128]{2,1,0:T(8,128)(2,1)S(1)} %pad_maximum_fusion.1.g0), channel_id=1, source_target_pairs={{0,4},{1,17},{2,6},{3,19},{4,0},{5,21},{6,2},{7,23},{8,12},{9,25},... | collective-permute-start | bytes 1966088 | tf_op jit(solution)/shard_map/ppermute | solution.py:264
  62.7 19.3 %collective-permute-start.17 = (bf16[4,640,128]{2,1,0:T(8,128)(2,1)S(1)}, bf16[4,640,128]{2,1,0:T(8,128)(2,1)S(1)}, u32[]{:S(2)}, u32[]{:S(2)}) collective-permute-start(bf16[4,640,128]{2,1,0:T(8,128)(2,1)S(1)} %pad_maximum_fusion.1.g0), channel_id=1, source_target_pairs={{0,6},{1,25},{2,0},{3,27},{4,2},{5,29},{6,4},{7,31},{8,14},{9,1},{... | collective-permute-start | bytes 1966088 | tf_op jit(solution)/shard_map/ppermute | solution.py:264
  77.5 19.5 %collective-permute-start.10 = (bf16[4,640,128]{2,1,0:T(8,128)(2,1)S(1)}, bf16[4,640,128]{2,1,0:T(8,128)(2,1)S(1)}, u32[]{:S(2)}, u32[]{:S(2)}) collective-permute-start(bf16[4,640,128]{2,1,0:T(8,128)(2,1)S(1)} %get-tuple-element.18), channel_id=1, source_target_pairs={{0,2},{1,9},{2,4},{3,11},{4,6},{5,13},{6,0},{7,15},{8,10},{9,17},{... | collective-permute-start | bytes 1966088 | tf_op jit(solution)/shard_map/ppermute | solution.py:264
  78.2 19.4 %collective-permute-start.11 = (bf16[4,640,128]{2,1,0:T(8,128)(2,1)S(1)}, bf16[4,640,128]{2,1,0:T(8,128)(2,1)S(1)}, u32[]{:S(2)}, u32[]{:S(2)}) collective-permute-start(bf16[4,640,128]{2,1,0:T(8,128)(2,1)S(1)} %get-tuple-element.19), channel_id=1, source_target_pairs={{0,4},{1,17},{2,6},{3,19},{4,0},{5,21},{6,2},{7,23},{8,12},{9,25},... | collective-permute-start | bytes 1966088 | tf_op jit(solution)/shard_map/ppermute | solution.py:264
  80.0 17.5 %collective-permute-start.9 = (bf16[4,640,128]{2,1,0:T(8,128)(2,1)S(1)}, bf16[4,640,128]{2,1,0:T(8,128)(2,1)S(1)}, u32[]{:S(2)}, u32[]{:S(2)}) collective-permute-start(bf16[4,640,128]{2,1,0:T(8,128)(2,1)S(1)} %get-tuple-element.17), channel_id=1, source_target_pairs={{0,6},{1,25},{2,0},{3,27},{4,2},{5,29},{6,4},{7,31},{8,14},{9,1},{... | collective-permute-start | bytes 1966088 | tf_op jit(solution)/shard_map/ppermute | solution.py:264
  95.4 12.5 %collective-permute-start.18 = (bf16[4,640,128]{2,1,0:T(8,128)(2,1)S(1)}, bf16[4,640,128]{2,1,0:T(8,128)(2,1)S(1)}, u32[]{:S(2)}, u32[]{:S(2)}) collective-permute-start(bf16[4,640,128]{2,1,0:T(8,128)(2,1)S(1)} %get-tuple-element.21), channel_id=1, source_target_pairs={{0,6},{1,25},{2,0},{3,27},{4,2},{5,29},{6,4},{7,31},{8,14},{9,1},{... | collective-permute-start | bytes 1966088 | tf_op jit(solution)/shard_map/ppermute | solution.py:264
  95.5 20.7 %collective-permute-start.19 = (bf16[4,640,128]{2,1,0:T(8,128)(2,1)S(1)}, bf16[4,640,128]{2,1,0:T(8,128)(2,1)S(1)}, u32[]{:S(2)}, u32[]{:S(2)}) collective-permute-start(bf16[4,640,128]{2,1,0:T(8,128)(2,1)S(1)} %get-tuple-element.22), channel_id=1, source_target_pairs={{0,2},{1,9},{2,4},{3,11},{4,6},{5,13},{6,0},{7,15},{8,10},{9,17},{... | collective-permute-start | bytes 1966088 | tf_op jit(solution)/shard_map/ppermute | solution.py:264
  97.0 19.3 %collective-permute-start.20 = (bf16[4,640,128]{2,1,0:T(8,128)(2,1)S(1)}, bf16[4,640,128]{2,1,0:T(8,128)(2,1)S(1)}, u32[]{:S(2)}, u32[]{:S(2)}) collective-permute-start(bf16[4,640,128]{2,1,0:T(8,128)(2,1)S(1)} %get-tuple-element.23), channel_id=1, source_target_pairs={{0,4},{1,17},{2,6},{3,19},{4,0},{5,21},{6,2},{7,23},{8,12},{9,25},... | collective-permute-start | bytes 1966088 | tf_op jit(solution)/shard_map/ppermute | solution.py:264
  98.0 28.1 %collective-permute-start.12 = (bf16[640,128]{1,0:T(8,128)(2,1)S(1)}, bf16[640,128]{1,0:T(8,128)(2,1)S(1)}, u32[]{:S(2)}, u32[]{:S(2)}) collective-permute-start(bf16[640,128]{1,0:T(8,128)(2,1)S(1)} %get-tuple-element.25), channel_id=1, source_target_pairs={{0,24},{1,7},{2,26},{3,1},{4,28},{5,3},{6,30},{7,5},{8,0},{9,15},{... | collective-permute-start | bytes 491528 | tf_op jit(solution)/shard_map/ppermute | solution.py:264
  107.9 21.0 %collective-permute-start.13 = (bf16[640,128]{1,0:T(8,128)(2,1)S(1)}, bf16[640,128]{1,0:T(8,128)(2,1)S(1)}, u32[]{:S(2)}, u32[]{:S(2)}) collective-permute-start(bf16[640,128]{1,0:T(8,128)(2,1)S(1)} %get-tuple-element.27), channel_id=1, source_target_pairs={{0,8},{1,3},{2,10},{3,5},{4,12},{5,7},{6,14},{7,1},{8,16},{9,11},{... | collective-permute-start | bytes 491528 | tf_op jit(solution)/shard_map/ppermute | solution.py:264
  107.9 21.0 %collective-permute-start.14 = (bf16[640,128]{1,0:T(8,128)(2,1)S(1)}, bf16[640,128]{1,0:T(8,128)(2,1)S(1)}, u32[]{:S(2)}, u32[]{:S(2)}) collective-permute-start(bf16[640,128]{1,0:T(8,128)(2,1)S(1)} %get-tuple-element.26), channel_id=1, source_target_pairs={{0,16},{1,5},{2,18},{3,7},{4,20},{5,1},{6,22},{7,3},{8,24},{9,13},... | collective-permute-start | bytes 491528 | tf_op jit(solution)/shard_map/ppermute | solution.py:264
  116.6 12.9 %collective-permute-start.21 = (bf16[640,128]{1,0:T(8,128)(2,1)S(1)}, bf16[640,128]{1,0:T(8,128)(2,1)S(1)}, u32[]{:S(2)}, u32[]{:S(2)}) collective-permute-start(bf16[640,128]{1,0:T(8,128)(2,1)S(1)} %get-tuple-element.28), channel_id=1, source_target_pairs={{0,24},{1,7},{2,26},{3,1},{4,28},{5,3},{6,30},{7,5},{8,0},{9,15},{... | collective-permute-start | bytes 491528 | tf_op jit(solution)/shard_map/ppermute | solution.py:264
  126.1 7.3 %collective-permute-start.23 = (bf16[640,128]{1,0:T(8,128)(2,1)S(1)}, bf16[640,128]{1,0:T(8,128)(2,1)S(1)}, u32[]{:S(2)}, u32[]{:S(2)}) collective-permute-start(bf16[640,128]{1,0:T(8,128)(2,1)S(1)} %get-tuple-element.29), channel_id=1, source_target_pairs={{0,16},{1,5},{2,18},{3,7},{4,20},{5,1},{6,22},{7,3},{8,24},{9,13},... | collective-permute-start | bytes 491528 | tf_op jit(solution)/shard_map/ppermute | solution.py:264
  134.8 23.9 %all-to-all-start.1 = ((bf16[16,80,128]{2,1,0:T(8,128)(2,1)}), bf16[16,80,128]{2,1,0:T(8,128)(2,1)S(1)}, u32[]{:S(2)}, u32[]{:S(2)}) async-start(bf16[16,80,128]{2,1,0:T(8,128)(2,1)} %pad_maximum_fusion.3), calls=%async_computation.1 | async-start | bytes 655360 | tf_op jit(solution)/shard_map/all_to_all | solution.py:218
  (5 other events, 24.6 us)

commit v2 on v1

--- a/solution.py
+++ b/solution.py
@@ -29,7 +29,7 @@
 
 
 def expert_kernel(where, g0, g1, g2, g3, wg0, wg1, wu0, wu1, wd0, wd1,
-                  p0, p1, p2, p3, rows_ref, hid_ref, gate_ref, held_ref, sems):
+                  p0, p1, p2, p3, rows_ref, hid_ref, gate_ref, held_ref, down_ref, sems):
     core = where[0]
     y = where[1]
     held = (g0, g1, g2, g3)
@@ -37,11 +37,14 @@
     blocks = rows_ref.shape[1] // (NY * LANES)
     n, width = g0.shape[1] // blocks, blocks * LANES
 
+    units = wd0.shape[0]
+    targets = [held_ref.at[i] for i in range(4)]
+    targets += [down_ref.at[pl.ds(i * units, units)] for i in range(2)]
     copies = [
-        pltpu.make_async_copy(src, held_ref.at[i], sems.at[i])
-        for i, src in enumerate((wg0, wu0, wg1, wu1, wd0, wd1))
+        pltpu.make_async_copy(src, dst, sems.at[i])
+        for i, (src, dst) in enumerate(zip((wg0, wu0, wg1, wu1, wd0, wd1), targets))
     ]
-    for copy in copies[:2]:
+    for copy in copies:
         copy.start()
 
     def columns(k):
@@ -72,7 +75,6 @@
             @pl.when(step == i)
             def _():
                 copies[i].wait()
-                copies[i + 2].start()
         value = lax.dot_general(
             rows_ref[...], held_ref[step], dims, preferred_element_type=jnp.float32
         )
@@ -84,15 +86,18 @@
         @pl.when(lax.rem(step, 2) == 1)
         def _():
             gate = gate_ref[...]
-            hid_ref[lax.div(step, 2)] = (gate / (1.0 + jnp.exp(-gate)) * value).astype(jnp.bfloat16)
+            hidden = (gate / (1.0 + jnp.exp(-gate)) * value).astype(jnp.bfloat16)
+            for i in range(2):
+                @pl.when(step == 2 * i + 1)
+                def _():
+                    hid_ref[:, i * units:(i + 1) * units] = hidden
 
     copies[4].wait()
     copies[5].wait()
 
     @pl.loop(0, 4)
     def _(k):
-        part = jnp.dot(hid_ref[0], held_ref[4, :, columns(k)], preferred_element_type=jnp.float32)
-        part += jnp.dot(hid_ref[1], held_ref[5, :, columns(k)], preferred_element_type=jnp.float32)
+        part = jnp.dot(hid_ref[...], down_ref[:, columns(k)], preferred_element_type=jnp.float32)
         part = part.astype(jnp.bfloat16)
         for i in range(4):
             @pl.when((core == 0) & (k == i))
@@ -118,9 +123,10 @@
         out_specs=[vmem] * 4,
         scratch_shapes=[
             pltpu.VMEM((4 * n, dim), jnp.bfloat16),
-            pltpu.VMEM((2, 4 * n, units), jnp.bfloat16),
+            pltpu.VMEM((4 * n, 2 * units), jnp.bfloat16),
             pltpu.VMEM((4 * n, units), jnp.float32),
-            pltpu.VMEM((6, units, dim), jnp.bfloat16),
+            pltpu.VMEM((4, units, dim), jnp.bfloat16),
+            pltpu.VMEM((2 * units, dim), jnp.bfloat16),
             pltpu.SemaphoreType.DMA((6,)),
         ],
         compiler_params=pltpu.CompilerParams(vmem_limit_bytes=48 * 1024 * 1024),
@@ -130,13 +136,18 @@
     )(where, *held, *weights)
 
 
-def dispatch_kernel(ids_ref, tokens_ref, sent_ref, spots_ref):
+def dispatch_kernel(ids_hbm, tokens_hbm, sent_ref, spots_ref, ids_ref, tokens_ref, sems):
+    ids_copy = pltpu.make_async_copy(ids_hbm, ids_ref, sems.at[0])
+    tokens_copy = pltpu.make_async_copy(tokens_hbm, tokens_ref, sems.at[1])
+    ids_copy.start()
+    tokens_copy.start()
     tok_rows, feat = tokens_ref.shape
     blocks = feat // LANES
     share = CAP // CHUNKS
     n = share // 2
     unit = blocks * n
     expert = lax.broadcasted_iota(jnp.int32, (EXPERTS, tok_rows), 0)
+    ids_copy.wait()
     named = [ids_ref[k:k + 1] == expert for k in range(2)]
     chosen = (named[0] | named[1]).astype(jnp.float32).astype(jnp.bfloat16)
     before = lax.broadcasted_iota(jnp.int32, (tok_rows, tok_rows), 0)
@@ -157,6 +168,7 @@
     sites = sent_ref.shape[0]
     site = lax.broadcasted_iota(jnp.int32, (sites, blocks * tok_rows), 0)
     picker = ((at[0] == site) | (at[1] == site)).astype(jnp.float32).astype(jnp.bfloat16)
+    tokens_copy.wait()
     tokens = jnp.concatenate(
         [tokens_ref[:, l * LANES:(l + 1) * LANES] for l in range(blocks)], axis=0
     )
@@ -172,9 +184,14 @@
             jax.ShapeDtypeStruct((EXPERTS * CAP * feat // LANES, LANES), jnp.bfloat16),
             jax.ShapeDtypeStruct((2, tok_rows), jnp.int32),
         ],
-        in_specs=[vmem] * 2,
+        in_specs=[pl.BlockSpec(memory_space=pltpu.HBM)] * 2,
         out_specs=[vmem] * 2,
-        compiler_params=pltpu.CompilerParams(vmem_limit_bytes=16 * 1024 * 1024),
+        scratch_shapes=[
+            pltpu.VMEM(ids.shape, ids.dtype),
+            pltpu.VMEM(tokens.shape, tokens.dtype),
+            pltpu.SemaphoreType.DMA((2,)),
+        ],
+        compiler_params=pltpu.CompilerParams(vmem_limit_bytes=64 * 1024 * 1024 - 65536),
     )(ids, tokens)
 
 
@@ -182,10 +199,10 @@
     n = CAP // CHUNKS // 2
     tok_rows = spots_ref.shape[0]
     site = lax.broadcasted_iota(jnp.int32, (tok_rows, take_ref.shape[2]), 1)
-    for k in range(take_ref.shape[0]):
-        for l in range(take_ref.shape[1] // tok_rows):
+    for k in range(2):
+        for l in range(take_ref.shape[0]):
             take = spots_ref[:, k:k + 1] + l * n == site
-            take_ref[k, l * tok_rows:(l + 1) * tok_rows] = (
+            take_ref[l, k * tok_rows:(k + 1) * tok_rows] = (
                 take.astype(jnp.float32).astype(jnp.bfloat16)
             )
 
@@ -193,13 +210,8 @@
 def combine_kernel(back_ref, take_ref, scores_ref, mixed_ref):
     tok_rows = mixed_ref.shape[0]
     for l in range(mixed_ref.shape[1] // LANES):
-        total = jnp.zeros((tok_rows, LANES), jnp.float32)
-        for k in range(2):
-            mine = jnp.dot(
-                take_ref[k, l * tok_rows:(l + 1) * tok_rows], back_ref[...],
-                preferred_element_type=jnp.float32,
-            )
-            total = total + scores_ref[:, k:k + 1] * mine
+        mine = jnp.dot(take_ref[l], back_ref[...], preferred_element_type=jnp.float32)
+        total = scores_ref[:, :1] * mine[:tok_rows] + scores_ref[:, 1:] * mine[tok_rows:]
         mixed_ref[:, l * LANES:(l + 1) * LANES] = total.astype(mixed_ref.dtype)
 
 
@@ -284,7 +296,7 @@
     tok_rows = tokens.shape[0]
     take = local_call(
         plan_kernel,
-        jax.ShapeDtypeStruct((2, blocks * tok_rows, CHUNKS * size), jnp.bfloat16),
+        jax.ShapeDtypeStruct((blocks, 2 * tok_rows, CHUNKS * size), jnp.bfloat16),
         spots,
     )
     return local_call(

time: 161 us -> 160 us (level)
  no operation moved by 1% of the time
where the time goes in v2:
time: 160 us
  starting transfers between devices  72.3 us (45%)
  waiting for transfers between devices  52.1 us (33%)
  Pallas kernels  31 us (19%)
  matrix products  2.09 us (1%)
  other arithmetic  1.73 us (1%)
    ppermute x21, starting transfers between devices, permute(): return lax.ppermute(v, PLANE, ring(axis, shift))  50.5 us
    ppermute x21, waiting for transfers between devices, permute(): return lax.ppermute(v, PLANE, ring(axis, shift))  27.3 us
    pallas_call x2, Pallas kernels, expert_part(): pl.pallas_call(expert_kernel, out_shape=[jax.ShapeDtypeStruct(held[0].sha...  26.2 us
    all_to_all x2, waiting for transfers between devices, exchange(): lax.all_to_all(v, ('z', 'c'), split_axis=0, concat_axis=0, tiled=True)  24.8 us
    all_to_all x2, starting transfers between devices, exchange(): lax.all_to_all(v, ('z', 'c'), split_axis=0, concat_axis=0, tiled=True)  21.1 us
  transfers between devices with their start and end apart: 26, of which 10 were waited for; matrix products, arithmetic and copies ran while one was open for 2% of the time, Pallas kernels for 17%

profile of v2, /device:TPU:1, one launch (start us, length us, event | category | flops | bytes accessed | tf_op | source)
XLA Modules:
  0.0 159.8 jit_solution(18032923974708724927)
XLA Ops:
  0.0 2.8 %shard_map.64 = (bf16[1280,128]{1,0:T(8,128)(2,1)}, s32[2,128]{1,0:T(2,128)}) custom-call(s32[2,128]{1,0:T(2,128)} %bitcast.52, bf16[128,512]{1,0:T(8,128)(2,1)} %tokens_hbm.1), custom_call_target="tpu_custom_call" | custom-call | tf_op jit(solution)/shard_map/pallas_call | solution.py:181
  2.8 10.0 %all-to-all-start = ((bf16[16,80,128]{2,1,0:T(8,128)(2,1)}), bf16[16,80,128]{2,1,0:T(8,128)(2,1)S(1)}, u32[]{:S(2)}, u32[]{:S(2)}) async-start(bf16[16,80,128]{2,1,0:T(8,128)(2,1)} %bitcast.47), calls=%async_computation | async-start | bytes 655360 | tf_op jit(solution)/shard_map/all_to_all | solution.py:230
  13.5 12.3 %all-to-all-done = bf16[16,80,128]{2,1,0:T(8,128)(2,1)S(1)} async-done(((bf16[16,80,128]{2,1,0:T(8,128)(2,1)}), bf16[16,80,128]{2,1,0:T(8,128)(2,1)S(1)}, u32[]{:S(2)}, u32[]{:S(2)}) %all-to-all-start) | async-done | bytes 327712 | tf_op jit(solution)/shard_map/all_to_all | solution.py:230
  28.0 2.6 %collective-permute-start.1 = (bf16[2,640,128]{2,1,0:T(8,128)(2,1)S(1)}, bf16[2,640,128]{2,1,0:T(8,128)(2,1)S(1)}, u32[]{:S(2)}, u32[]{:S(2)}) collective-permute-start(bf16[2,640,128]{2,1,0:T(8,128)(2,1)S(1)} %pad_maximum_fusion.2), channel_id=1, source_target_pairs={{0,16},{1,5},{2,18},{3,7},{4,20},{5,1},{6,22},{7,3},{8,24},{9,13},... | collective-permute-start | bytes 983048 | tf_op jit(solution)/shard_map/ppermute | solution.py:276
  30.6 3.5 %collective-permute-done = bf16[2,640,128]{2,1,0:T(8,128)(2,1)S(1)} collective-permute-done((bf16[2,640,128]{2,1,0:T(8,128)(2,1)S(1)}, bf16[2,640,128]{2,1,0:T(8,128)(2,1)S(1)}, u32[]{:S(2)}, u32[]{:S(2)}) %collective-permute-start) | collective-permute-done | bytes 327712 | tf_op jit(solution)/shard_map/ppermute | solution.py:276
  34.1 1.5 collective-permute-start.2
  35.7 2.9 %collective-permute-done.1 = bf16[2,640,128]{2,1,0:T(8,128)(2,1)S(1)} collective-permute-done((bf16[2,640,128]{2,1,0:T(8,128)(2,1)S(1)}, bf16[2,640,128]{2,1,0:T(8,128)(2,1)S(1)}, u32[]{:S(2)}, u32[]{:S(2)}) %collective-permute-start.1) | collective-permute-done | bytes 327712 | tf_op jit(solution)/shard_map/ppermute | solution.py:276
  38.6 1.7 %collective-permute-done.2 = bf16[2,640,128]{2,1,0:T(8,128)(2,1)S(1)} collective-permute-done((bf16[2,640,128]{2,1,0:T(8,128)(2,1)S(1)}, bf16[2,640,128]{2,1,0:T(8,128)(2,1)S(1)}, u32[]{:S(2)}, u32[]{:S(2)}) %collective-permute-start.2) | collective-permute-done | bytes 327712 | tf_op jit(solution)/shard_map/ppermute | solution.py:276
  41.4 2.9 %collective-permute-start.4 = (bf16[4,640,128]{2,1,0:T(8,128)(2,1)S(1)}, bf16[4,640,128]{2,1,0:T(8,128)(2,1)S(1)}, u32[]{:S(2)}, u32[]{:S(2)}) collective-permute-start(bf16[4,640,128]{2,1,0:T(8,128)(2,1)S(1)} %pad_maximum_fusion.g0), channel_id=1, source_target_pairs={{0,4},{1,17},{2,6},{3,19},{4,0},{5,21},{6,2},{7,23},{8,12},{9,25},... | collective-permute-start | bytes 1966088 | tf_op jit(solution)/shard_map/ppermute | solution.py:276
  44.3 7.2 %collective-permute-done.3.g1 = bf16[4,640,128]{2,1,0:T(8,128)(2,1)S(1)} collective-permute-done((bf16[4,640,128]{2,1,0:T(8,128)(2,1)S(1)}, bf16[4,640,128]{2,1,0:T(8,128)(2,1)S(1)}, u32[]{:S(2)}, u32[]{:S(2)}) %collective-permute-start.3) | collective-permute-done | bytes 655392 | tf_op jit(solution)/shard_map/ppermute | solution.py:276
  53.0 6.6 %collective-permute-done.4.g2 = bf16[4,640,128]{2,1,0:T(8,128)(2,1)S(1)} collective-permute-done((bf16[4,640,128]{2,1,0:T(8,128)(2,1)S(1)}, bf16[4,640,128]{2,1,0:T(8,128)(2,1)S(1)}, u32[]{:S(2)}, u32[]{:S(2)}) %collective-permute-start.4) | collective-permute-done | bytes 655392 | tf_op jit(solution)/shard_map/ppermute | solution.py:276
  59.6 1.6 %collective-permute-done.5.g3 = bf16[4,640,128]{2,1,0:T(8,128)(2,1)S(1)} collective-permute-done((bf16[4,640,128]{2,1,0:T(8,128)(2,1)S(1)}, bf16[4,640,128]{2,1,0:T(8,128)(2,1)S(1)}, u32[]{:S(2)}, u32[]{:S(2)}) %collective-permute-start.5) | collective-permute-done | bytes 655392 | tf_op jit(solution)/shard_map/ppermute | solution.py:276
  63.8 13.1 %shard_map.65 = (bf16[4,640,128]{2,1,0:T(8,128)(2,1)S(1)}, bf16[4,640,128]{2,1,0:T(8,128)(2,1)S(1)}, bf16[4,640,128]{2,1,0:T(8,128)(2,1)S(1)}, bf16[4,640,128]{2,1,0:T(8,128)(2,1)S(1)}) custom-call(s32[2]{0:T(128)S(1)} %pad_add_fusion.where, bf16[4,640,128]{2,1,0:T(8,128)(2,1)S(1)} %pad_maximum_fusion.g0, ...), custom_call_target="tpu_custom_call" | custom-call | flops 7046430720 | bytes 31457280 | tf_op jit(solution)/shard_map/pallas_call | solution.py:118
  77.6 1.9 %collective-permute-start.11 = (bf16[4,640,128]{2,1,0:T(8,128)(2,1)S(1)}, bf16[4,640,128]{2,1,0:T(8,128)(2,1)S(1)}, u32[]{:S(2)}, u32[]{:S(2)}) collective-permute-start(bf16[4,640,128]{2,1,0:T(8,128)(2,1)S(1)} %get-tuple-element.19), channel_id=1, source_target_pairs={{0,4},{1,17},{2,6},{3,19},{4,0},{5,21},{6,2},{7,23},{8,12},{9,25},... | collective-permute-start | bytes 1966088 | tf_op jit(solution)/shard_map/ppermute | solution.py:276
  79.5 2.0 %collective-permute-start.9 = (bf16[4,640,128]{2,1,0:T(8,128)(2,1)S(1)}, bf16[4,640,128]{2,1,0:T(8,128)(2,1)S(1)}, u32[]{:S(2)}, u32[]{:S(2)}) collective-permute-start(bf16[4,640,128]{2,1,0:T(8,128)(2,1)S(1)} %get-tuple-element.17), channel_id=1, source_target_pairs={{0,6},{1,25},{2,0},{3,27},{4,2},{5,29},{6,4},{7,31},{8,14},{9,1},{... | collective-permute-start | bytes 1966088 | tf_op jit(solution)/shard_map/ppermute | solution.py:276
  81.4 13.1 %shard_map.66 = (bf16[4,640,128]{2,1,0:T(8,128)(2,1)S(1)}, bf16[4,640,128]{2,1,0:T(8,128)(2,1)S(1)}, bf16[4,640,128]{2,1,0:T(8,128)(2,1)S(1)}, bf16[4,640,128]{2,1,0:T(8,128)(2,1)S(1)}) custom-call(s32[2]{0:T(128)S(1)} %pad_add_fusion.where, bf16[4,640,128]{2,1,0:T(8,128)(2,1)S(1)} %pad_maximum_fusion.1.g0, ...), custom_call_target="tpu_custom_call" | custom-call | flops 7046430720 | bytes 31457280 | tf_op jit(solution)/shard_map/pallas_call | solution.py:118
  97.1 9.9 %collective-permute-start.12 = (bf16[640,128]{1,0:T(8,128)(2,1)S(1)}, bf16[640,128]{1,0:T(8,128)(2,1)S(1)}, u32[]{:S(2)}, u32[]{:S(2)}) collective-permute-start(bf16[640,128]{1,0:T(8,128)(2,1)S(1)} %get-tuple-element.25), channel_id=1, source_target_pairs={{0,24},{1,7},{2,26},{3,1},{4,28},{5,3},{6,30},{7,5},{8,0},{9,15},{... | collective-permute-start | bytes 491528 | tf_op jit(solution)/shard_map/ppermute | solution.py:276
  107.1 8.3 %collective-permute-start.14 = (bf16[640,128]{1,0:T(8,128)(2,1)S(1)}, bf16[640,128]{1,0:T(8,128)(2,1)S(1)}, u32[]{:S(2)}, u32[]{:S(2)}) collective-permute-start(bf16[640,128]{1,0:T(8,128)(2,1)S(1)} %get-tuple-element.26), channel_id=1, source_target_pairs={{0,16},{1,5},{2,18},{3,7},{4,20},{5,1},{6,22},{7,3},{8,24},{9,13},... | collective-permute-start | bytes 491528 | tf_op jit(solution)/shard_map/ppermute | solution.py:276
  115.8 8.3 %collective-permute-start.21 = (bf16[640,128]{1,0:T(8,128)(2,1)S(1)}, bf16[640,128]{1,0:T(8,128)(2,1)S(1)}, u32[]{:S(2)}, u32[]{:S(2)}) collective-permute-start(bf16[640,128]{1,0:T(8,128)(2,1)S(1)} %get-tuple-element.28), channel_id=1, source_target_pairs={{0,24},{1,7},{2,26},{3,1},{4,28},{5,3},{6,30},{7,5},{8,0},{9,15},{... | collective-permute-start | bytes 491528 | tf_op jit(solution)/shard_map/ppermute | solution.py:276
  125.1 3.0 %collective-permute-start.23 = (bf16[640,128]{1,0:T(8,128)(2,1)S(1)}, bf16[640,128]{1,0:T(8,128)(2,1)S(1)}, u32[]{:S(2)}, u32[]{:S(2)}) collective-permute-start(bf16[640,128]{1,0:T(8,128)(2,1)S(1)} %get-tuple-element.29), channel_id=1, source_target_pairs={{0,16},{1,5},{2,18},{3,7},{4,20},{5,1},{6,22},{7,3},{8,24},{9,13},... | collective-permute-start | bytes 491528 | tf_op jit(solution)/shard_map/ppermute | solution.py:276
  129.6 2.9 %collective-permute-done.23 = bf16[640,128]{1,0:T(8,128)(2,1)S(1)} collective-permute-done((bf16[640,128]{1,0:T(8,128)(2,1)S(1)}, bf16[640,128]{1,0:T(8,128)(2,1)S(1)}, u32[]{:S(2)}, u32[]{:S(2)}) %collective-permute-start.23) | collective-permute-done | bytes 163872 | tf_op jit(solution)/shard_map/ppermute | solution.py:276
  133.9 11.1 %all-to-all-start.1 = ((bf16[16,80,128]{2,1,0:T(8,128)(2,1)}), bf16[16,80,128]{2,1,0:T(8,128)(2,1)S(1)}, u32[]{:S(2)}, u32[]{:S(2)}) async-start(bf16[16,80,128]{2,1,0:T(8,128)(2,1)} %pad_maximum_fusion.3), calls=%async_computation.1 | async-start | bytes 655360 | tf_op jit(solution)/shard_map/all_to_all | solution.py:230
  145.8 12.5 %all-to-all-done.1 = bf16[16,80,128]{2,1,0:T(8,128)(2,1)S(1)} async-done(((bf16[16,80,128]{2,1,0:T(8,128)(2,1)}), bf16[16,80,128]{2,1,0:T(8,128)(2,1)S(1)}, u32[]{:S(2)}, u32[]{:S(2)}) %all-to-all-start.1) | async-done | bytes 327712 | tf_op jit(solution)/shard_map/all_to_all | solution.py:230
  158.3 1.5 shard_map.68
  (57 shorter events, 16.4 us)
Async XLA Ops:
  2.8 23.0 %all-to-all-start = ((bf16[16,80,128]{2,1,0:T(8,128)(2,1)}), bf16[16,80,128]{2,1,0:T(8,128)(2,1)S(1)}, u32[]{:S(2)}, u32[]{:S(2)}) async-start(bf16[16,80,128]{2,1,0:T(8,128)(2,1)} %bitcast.47), calls=%async_computation | async-start | bytes 655360 | tf_op jit(solution)/shard_map/all_to_all | solution.py:230
  12.8 49.6 %collective-permute-start.6 = (bf16[448,4096]{1,0:T(8,128)(2,1)}, bf16[448,4096]{1,0:T(8,128)(2,1)}, u32[]{:S(2)}, u32[]{:S(2)}) collective-permute-start(bf16[448,4096]{1,0:T(8,128)(2,1)} %bitcast.53), channel_id=1, source_target_pairs={{0,1},{1,0},{2,3},{3,2},{4,5},{5,4},{6,7},{7,6},{8,9},{9,8},{10,11... | collective-permute-start | bytes 11010056 | tf_op jit(solution)/shard_map/ppermute | solution.py:249
  13.0 50.8 %collective-permute-start.7 = (bf16[448,4096]{1,0:T(8,128)(2,1)}, bf16[448,4096]{1,0:T(8,128)(2,1)}, u32[]{:S(2)}, u32[]{:S(2)}) collective-permute-start(bf16[448,4096]{1,0:T(8,128)(2,1)} %bitcast.56), channel_id=1, source_target_pairs={{0,1},{1,0},{2,3},{3,2},{4,5},{5,4},{6,7},{7,6},{8,9},{9,8},{10,11... | collective-permute-start | bytes 11010056 | tf_op jit(solution)/shard_map/ppermute | solution.py:249
  13.3 50.5 %collective-permute-start.8 = (bf16[448,4096]{1,0:T(8,128)(2,1)}, bf16[448,4096]{1,0:T(8,128)(2,1)}, u32[]{:S(2)}, u32[]{:S(2)}) collective-permute-start(bf16[448,4096]{1,0:T(8,128)(2,1)} %bitcast.59), channel_id=1, source_target_pairs={{0,1},{1,0},{2,3},{3,2},{4,5},{5,4},{6,7},{7,6},{8,9},{9,8},{10,11... | collective-permute-start | bytes 11010056 | tf_op jit(solution)/shard_map/ppermute | solution.py:249
  26.6 7.5 %collective-permute-start = (bf16[2,640,128]{2,1,0:T(8,128)(2,1)S(1)}, bf16[2,640,128]{2,1,0:T(8,128)(2,1)S(1)}, u32[]{:S(2)}, u32[]{:S(2)}) collective-permute-start(bf16[2,640,128]{2,1,0:T(8,128)(2,1)S(1)} %pad_maximum_fusion.2), channel_id=1, source_target_pairs={{0,8},{1,3},{2,10},{3,5},{4,12},{5,7},{6,14},{7,1},{8,16},{9,11},{... | collective-permute-start | bytes 983048 | tf_op jit(solution)/shard_map/ppermute | solution.py:276
  28.0 10.6 %collective-permute-start.1 = (bf16[2,640,128]{2,1,0:T(8,128)(2,1)S(1)}, bf16[2,640,128]{2,1,0:T(8,128)(2,1)S(1)}, u32[]{:S(2)}, u32[]{:S(2)}) collective-permute-start(bf16[2,640,128]{2,1,0:T(8,128)(2,1)S(1)} %pad_maximum_fusion.2), channel_id=1, source_target_pairs={{0,16},{1,5},{2,18},{3,7},{4,20},{5,1},{6,22},{7,3},{8,24},{9,13},... | collective-permute-start | bytes 983048 | tf_op jit(solution)/shard_map/ppermute | solution.py:276
  40.5 11.0 %collective-permute-start.3 = (bf16[4,640,128]{2,1,0:T(8,128)(2,1)S(1)}, bf16[4,640,128]{2,1,0:T(8,128)(2,1)S(1)}, u32[]{:S(2)}, u32[]{:S(2)}) collective-permute-start(bf16[4,640,128]{2,1,0:T(8,128)(2,1)S(1)} %pad_maximum_fusion.g0), channel_id=1, source_target_pairs={{0,2},{1,9},{2,4},{3,11},{4,6},{5,13},{6,0},{7,15},{8,10},{9,17},{... | collective-permute-start | bytes 1966088 | tf_op jit(solution)/shard_map/ppermute | solution.py:276
  41.4 18.2 %collective-permute-start.4 = (bf16[4,640,128]{2,1,0:T(8,128)(2,1)S(1)}, bf16[4,640,128]{2,1,0:T(8,128)(2,1)S(1)}, u32[]{:S(2)}, u32[]{:S(2)}) collective-permute-start(bf16[4,640,128]{2,1,0:T(8,128)(2,1)S(1)} %pad_maximum_fusion.g0), channel_id=1, source_target_pairs={{0,4},{1,17},{2,6},{3,19},{4,0},{5,21},{6,2},{7,23},{8,12},{9,25},... | collective-permute-start | bytes 1966088 | tf_op jit(solution)/shard_map/ppermute | solution.py:276
  51.5 9.7 %collective-permute-start.5 = (bf16[4,640,128]{2,1,0:T(8,128)(2,1)S(1)}, bf16[4,640,128]{2,1,0:T(8,128)(2,1)S(1)}, u32[]{:S(2)}, u32[]{:S(2)}) collective-permute-start(bf16[4,640,128]{2,1,0:T(8,128)(2,1)S(1)} %pad_maximum_fusion.g0), channel_id=1, source_target_pairs={{0,6},{1,25},{2,0},{3,27},{4,2},{5,29},{6,4},{7,31},{8,14},{9,1},{... | collective-permute-start | bytes 1966088 | tf_op jit(solution)/shard_map/ppermute | solution.py:276
  59.6 19.9 %collective-permute-start.15 = (bf16[4,640,128]{2,1,0:T(8,128)(2,1)S(1)}, bf16[4,640,128]{2,1,0:T(8,128)(2,1)S(1)}, u32[]{:S(2)}, u32[]{:S(2)}) collective-permute-start(bf16[4,640,128]{2,1,0:T(8,128)(2,1)S(1)} %pad_maximum_fusion.1.g0), channel_id=1, source_target_pairs={{0,2},{1,9},{2,4},{3,11},{4,6},{5,13},{6,0},{7,15},{8,10},{9,17},{... | collective-permute-start | bytes 1966088 | tf_op jit(solution)/shard_map/ppermute | solution.py:276
  61.2 20.2 %collective-permute-start.16 = (bf16[4,640,128]{2,1,0:T(8,128)(2,1)S(1)}, bf16[4,640,128]{2,1,0:T(8,128)(2,1)S(1)}, u32[]{:S(2)}, u32[]{:S(2)}) collective-permute-start(bf16[4,640,128]{2,1,0:T(8,128)(2,1)S(1)} %pad_maximum_fusion.1.g0), channel_id=1, source_target_pairs={{0,4},{1,17},{2,6},{3,19},{4,0},{5,21},{6,2},{7,23},{8,12},{9,25},... | collective-permute-start | bytes 1966088 | tf_op jit(solution)/shard_map/ppermute | solution.py:276
  62.4 19.0 %collective-permute-start.17 = (bf16[4,640,128]{2,1,0:T(8,128)(2,1)S(1)}, bf16[4,640,128]{2,1,0:T(8,128)(2,1)S(1)}, u32[]{:S(2)}, u32[]{:S(2)}) collective-permute-start(bf16[4,640,128]{2,1,0:T(8,128)(2,1)S(1)} %pad_maximum_fusion.1.g0), channel_id=1, source_target_pairs={{0,6},{1,25},{2,0},{3,27},{4,2},{5,29},{6,4},{7,31},{8,14},{9,1},{... | collective-permute-start | bytes 1966088 | tf_op jit(solution)/shard_map/ppermute | solution.py:276
  76.9 19.2 %collective-permute-start.10 = (bf16[4,640,128]{2,1,0:T(8,128)(2,1)S(1)}, bf16[4,640,128]{2,1,0:T(8,128)(2,1)S(1)}, u32[]{:S(2)}, u32[]{:S(2)}) collective-permute-start(bf16[4,640,128]{2,1,0:T(8,128)(2,1)S(1)} %get-tuple-element.18), channel_id=1, source_target_pairs={{0,2},{1,9},{2,4},{3,11},{4,6},{5,13},{6,0},{7,15},{8,10},{9,17},{... | collective-permute-start | bytes 1966088 | tf_op jit(solution)/shard_map/ppermute | solution.py:276
  77.6 19.1 %collective-permute-start.11 = (bf16[4,640,128]{2,1,0:T(8,128)(2,1)S(1)}, bf16[4,640,128]{2,1,0:T(8,128)(2,1)S(1)}, u32[]{:S(2)}, u32[]{:S(2)}) collective-permute-start(bf16[4,640,128]{2,1,0:T(8,128)(2,1)S(1)} %get-tuple-element.19), channel_id=1, source_target_pairs={{0,4},{1,17},{2,6},{3,19},{4,0},{5,21},{6,2},{7,23},{8,12},{9,25},... | collective-permute-start | bytes 1966088 | tf_op jit(solution)/shard_map/ppermute | solution.py:276
  79.5 17.3 %collective-permute-start.9 = (bf16[4,640,128]{2,1,0:T(8,128)(2,1)S(1)}, bf16[4,640,128]{2,1,0:T(8,128)(2,1)S(1)}, u32[]{:S(2)}, u32[]{:S(2)}) collective-permute-start(bf16[4,640,128]{2,1,0:T(8,128)(2,1)S(1)} %get-tuple-element.17), channel_id=1, source_target_pairs={{0,6},{1,25},{2,0},{3,27},{4,2},{5,29},{6,4},{7,31},{8,14},{9,1},{... | collective-permute-start | bytes 1966088 | tf_op jit(solution)/shard_map/ppermute | solution.py:276
  94.6 12.5 %collective-permute-start.18 = (bf16[4,640,128]{2,1,0:T(8,128)(2,1)S(1)}, bf16[4,640,128]{2,1,0:T(8,128)(2,1)S(1)}, u32[]{:S(2)}, u32[]{:S(2)}) collective-permute-start(bf16[4,640,128]{2,1,0:T(8,128)(2,1)S(1)} %get-tuple-element.21), channel_id=1, source_target_pairs={{0,6},{1,25},{2,0},{3,27},{4,2},{5,29},{6,4},{7,31},{8,14},{9,1},{... | collective-permute-start | bytes 1966088 | tf_op jit(solution)/shard_map/ppermute | solution.py:276
  95.0 20.5 %collective-permute-start.19 = (bf16[4,640,128]{2,1,0:T(8,128)(2,1)S(1)}, bf16[4,640,128]{2,1,0:T(8,128)(2,1)S(1)}, u32[]{:S(2)}, u32[]{:S(2)}) collective-permute-start(bf16[4,640,128]{2,1,0:T(8,128)(2,1)S(1)} %get-tuple-element.22), channel_id=1, source_target_pairs={{0,2},{1,9},{2,4},{3,11},{4,6},{5,13},{6,0},{7,15},{8,10},{9,17},{... | collective-permute-start | bytes 1966088 | tf_op jit(solution)/shard_map/ppermute | solution.py:276
  96.1 19.3 %collective-permute-start.20 = (bf16[4,640,128]{2,1,0:T(8,128)(2,1)S(1)}, bf16[4,640,128]{2,1,0:T(8,128)(2,1)S(1)}, u32[]{:S(2)}, u32[]{:S(2)}) collective-permute-start(bf16[4,640,128]{2,1,0:T(8,128)(2,1)S(1)} %get-tuple-element.23), channel_id=1, source_target_pairs={{0,4},{1,17},{2,6},{3,19},{4,0},{5,21},{6,2},{7,23},{8,12},{9,25},... | collective-permute-start | bytes 1966088 | tf_op jit(solution)/shard_map/ppermute | solution.py:276
  97.1 28.0 %collective-permute-start.12 = (bf16[640,128]{1,0:T(8,128)(2,1)S(1)}, bf16[640,128]{1,0:T(8,128)(2,1)S(1)}, u32[]{:S(2)}, u32[]{:S(2)}) collective-permute-start(bf16[640,128]{1,0:T(8,128)(2,1)S(1)} %get-tuple-element.25), channel_id=1, source_target_pairs={{0,24},{1,7},{2,26},{3,1},{4,28},{5,3},{6,30},{7,5},{8,0},{9,15},{... | collective-permute-start | bytes 491528 | tf_op jit(solution)/shard_map/ppermute | solution.py:276
  107.0 21.0 %collective-permute-start.13 = (bf16[640,128]{1,0:T(8,128)(2,1)S(1)}, bf16[640,128]{1,0:T(8,128)(2,1)S(1)}, u32[]{:S(2)}, u32[]{:S(2)}) collective-permute-start(bf16[640,128]{1,0:T(8,128)(2,1)S(1)} %get-tuple-element.27), channel_id=1, source_target_pairs={{0,8},{1,3},{2,10},{3,5},{4,12},{5,7},{6,14},{7,1},{8,16},{9,11},{... | collective-permute-start | bytes 491528 | tf_op jit(solution)/shard_map/ppermute | solution.py:276
  107.1 21.0 %collective-permute-start.14 = (bf16[640,128]{1,0:T(8,128)(2,1)S(1)}, bf16[640,128]{1,0:T(8,128)(2,1)S(1)}, u32[]{:S(2)}, u32[]{:S(2)}) collective-permute-start(bf16[640,128]{1,0:T(8,128)(2,1)S(1)} %get-tuple-element.26), channel_id=1, source_target_pairs={{0,16},{1,5},{2,18},{3,7},{4,20},{5,1},{6,22},{7,3},{8,24},{9,13},... | collective-permute-start | bytes 491528 | tf_op jit(solution)/shard_map/ppermute | solution.py:276
  115.8 12.9 %collective-permute-start.21 = (bf16[640,128]{1,0:T(8,128)(2,1)S(1)}, bf16[640,128]{1,0:T(8,128)(2,1)S(1)}, u32[]{:S(2)}, u32[]{:S(2)}) collective-permute-start(bf16[640,128]{1,0:T(8,128)(2,1)S(1)} %get-tuple-element.28), channel_id=1, source_target_pairs={{0,24},{1,7},{2,26},{3,1},{4,28},{5,3},{6,30},{7,5},{8,0},{9,15},{... | collective-permute-start | bytes 491528 | tf_op jit(solution)/shard_map/ppermute | solution.py:276
  125.1 7.4 %collective-permute-start.23 = (bf16[640,128]{1,0:T(8,128)(2,1)S(1)}, bf16[640,128]{1,0:T(8,128)(2,1)S(1)}, u32[]{:S(2)}, u32[]{:S(2)}) collective-permute-start(bf16[640,128]{1,0:T(8,128)(2,1)S(1)} %get-tuple-element.29), channel_id=1, source_target_pairs={{0,16},{1,5},{2,18},{3,7},{4,20},{5,1},{6,22},{7,3},{8,24},{9,13},... | collective-permute-start | bytes 491528 | tf_op jit(solution)/shard_map/ppermute | solution.py:276
  133.9 24.4 %all-to-all-start.1 = ((bf16[16,80,128]{2,1,0:T(8,128)(2,1)}), bf16[16,80,128]{2,1,0:T(8,128)(2,1)S(1)}, u32[]{:S(2)}, u32[]{:S(2)}) async-start(bf16[16,80,128]{2,1,0:T(8,128)(2,1)} %pad_maximum_fusion.3), calls=%async_computation.1 | async-start | bytes 655360 | tf_op jit(solution)/shard_map/all_to_all | solution.py:230
  (4 other events, 39.9 us)

commit v3 on v2

--- a/solution.py
+++ b/solution.py
@@ -29,7 +29,7 @@
 
 
 def expert_kernel(where, g0, g1, g2, g3, wg0, wg1, wu0, wu1, wd0, wd1,
-                  p0, p1, p2, p3, rows_ref, hid_ref, gate_ref, held_ref, down_ref, sems):
+                  p0, p1, p2, p3, rows_ref, hid_ref, gate_ref, held_ref, sems):
     core = where[0]
     y = where[1]
     held = (g0, g1, g2, g3)
@@ -37,12 +37,9 @@
     blocks = rows_ref.shape[1] // (NY * LANES)
     n, width = g0.shape[1] // blocks, blocks * LANES
 
-    units = wd0.shape[0]
-    targets = [held_ref.at[i] for i in range(4)]
-    targets += [down_ref.at[pl.ds(i * units, units)] for i in range(2)]
     copies = [
-        pltpu.make_async_copy(src, dst, sems.at[i])
-        for i, (src, dst) in enumerate(zip((wg0, wu0, wg1, wu1, wd0, wd1), targets))
+        pltpu.make_async_copy(src, held_ref.at[i], sems.at[i])
+        for i, src in enumerate((wg0, wu0, wg1, wu1, wd0, wd1))
     ]
     for copy in copies:
         copy.start()
@@ -86,18 +83,15 @@
         @pl.when(lax.rem(step, 2) == 1)
         def _():
             gate = gate_ref[...]
-            hidden = (gate / (1.0 + jnp.exp(-gate)) * value).astype(jnp.bfloat16)
-            for i in range(2):
-                @pl.when(step == 2 * i + 1)
-                def _():
-                    hid_ref[:, i * units:(i + 1) * units] = hidden
+            hid_ref[lax.div(step, 2)] = (gate / (1.0 + jnp.exp(-gate)) * value).astype(jnp.bfloat16)
 
     copies[4].wait()
     copies[5].wait()
 
     @pl.loop(0, 4)
     def _(k):
-        part = jnp.dot(hid_ref[...], down_ref[:, columns(k)], preferred_element_type=jnp.float32)
+        part = jnp.dot(hid_ref[0], held_ref[4, :, columns(k)], preferred_element_type=jnp.float32)
+        part += jnp.dot(hid_ref[1], held_ref[5, :, columns(k)], preferred_element_type=jnp.float32)
         part = part.astype(jnp.bfloat16)
         for i in range(4):
             @pl.when((core == 0) & (k == i))
@@ -118,22 +112,38 @@
     return pl.pallas_call(
         expert_kernel,
         out_shape=[jax.ShapeDtypeStruct(held[0].shape, jnp.bfloat16)] * 4,
-        in_specs=[pl.BlockSpec(memory_space=pltpu.SMEM)] + [vmem] * 4
-        + [pl.BlockSpec(memory_space=pltpu.HBM)] * 6,
+        in_specs=[pl.BlockSpec(memory_space=pltpu.SMEM)] + [vmem] * 5
+        + [pl.BlockSpec(memory_space=pltpu.HBM)] * 5,
         out_specs=[vmem] * 4,
         scratch_shapes=[
             pltpu.VMEM((4 * n, dim), jnp.bfloat16),
-            pltpu.VMEM((4 * n, 2 * units), jnp.bfloat16),
+            pltpu.VMEM((2, 4 * n, units), jnp.bfloat16),
             pltpu.VMEM((4 * n, units), jnp.float32),
-            pltpu.VMEM((4, units, dim), jnp.bfloat16),
-            pltpu.VMEM((2 * units, dim), jnp.bfloat16),
+            pltpu.VMEM((6, units, dim), jnp.bfloat16),
             pltpu.SemaphoreType.DMA((6,)),
         ],
-        compiler_params=pltpu.CompilerParams(vmem_limit_bytes=48 * 1024 * 1024),
+        compiler_params=pltpu.CompilerParams(vmem_limit_bytes=44 * 1024 * 1024),
         cost_estimate=pl.CostEstimate(
             flops=2 * 4 * n * dim * units * 6, bytes_accessed=30 << 20, transcendentals=0
         ),
     )(where, *held, *weights)
+
+
+def hold_kernel(src_ref, dst_ref, sem):
+    copy = pltpu.make_async_copy(src_ref, dst_ref, sem)
+    copy.start()
+    copy.wait()
+
+
+def hold(weight):
+    return pl.pallas_call(
+        hold_kernel,
+        out_shape=pltpu.VMEM(weight.shape, weight.dtype),
+        in_specs=[pl.BlockSpec(memory_space=pltpu.HBM)],
+        out_specs=pl.BlockSpec(memory_space=pltpu.VMEM),
+        scratch_shapes=[pltpu.SemaphoreType.DMA],
+        compiler_params=pltpu.CompilerParams(vmem_limit_bytes=8 * 1024 * 1024),
+    )(weight)
 
 
 def dispatch_kernel(ids_hbm, tokens_hbm, sent_ref, spots_ref, ids_ref, tokens_ref, sems):
@@ -280,8 +290,11 @@
     held = []
     for i in range(CHUNKS):
         first = jnp.stack([here[i]] + [near[s][i] for s in (1, 2, 3)])
-        far = {s: permute(first, 1, s) for s in order}
+        far = {}
+        for s in order:
+            far[s] = permute(first, 1, s)
         held.append((first, far[1], far[2], far[3]))
+    weights[0] = hold(weights[0])
     parts = [expert_part(where, h, weights) for h in held]
 
     backs = []

time: 160 us -> 160 us (level)
  local copies, waits for them, and re-layouts: 0.4 us -> 6.37 us
  waiting for transfers between devices: 52.1 us -> 48 us
  Pallas kernels: 31 us -> 28.8 us
    unnamed x5 -> x11, local copies, waits for them, and re-layouts: 0.12 us -> 6.09 us
    ppermute x21, waiting for transfers between devices: 27.3 us -> 23.3 us  [permute(): return lax.ppermute(v, PLANE, ring(axis, shift))]
    pallas_call x2, Pallas kernels: 26.2 us -> 23.8 us  [expert_part(): pl.pallas_call(expert_kernel, out_shape=[jax.ShapeDtypeStruct(held[0].sha...]
  transfers between devices with their start and end apart: 26 -> 26, of which waited for: 10 -> 11; matrix products, arithmetic and copies ran while one was open for 2% -> 2% of each run, Pallas kernels for 17% -> 15%
where the time goes in v3:
time: 160 us; the launch traced here: 159 us
  starting transfers between devices  72.1 us (45%)
  waiting for transfers between devices  48 us (30%)
  Pallas kernels  28.8 us (18%)
  local copies, waits for them, and re-layouts  6.37 us (4%)
  matrix products  2.09 us (1%)
  other arithmetic  1.74 us (1%)
    ppermute x21, starting transfers between devices, permute(): return lax.ppermute(v, PLANE, ring(axis, shift))  50.8 us
    all_to_all x2, waiting for transfers between devices, exchange(): lax.all_to_all(v, ('z', 'c'), split_axis=0, concat_axis=0, tiled=True)  24.8 us
    pallas_call x2, Pallas kernels, expert_part(): pl.pallas_call(expert_kernel, out_shape=[jax.ShapeDtypeStruct(held[0].sha...  23.8 us
    ppermute x21, waiting for transfers between devices, permute(): return lax.ppermute(v, PLANE, ring(axis, shift))  23.3 us
    all_to_all x2, starting transfers between devices, exchange(): lax.all_to_all(v, ('z', 'c'), split_axis=0, concat_axis=0, tiled=True)  20.7 us
    unnamed x11, local copies, waits for them, and re-layouts  6.09 us
  transfers between devices with their start and end apart: 26, of which 11 were waited for; matrix products, arithmetic and copies ran while one was open for 2% of the time, Pallas kernels for 15%

profile of v3, /device:TPU:1, one launch (start us, length us, event | category | flops | bytes accessed | tf_op | source)
XLA Modules:
  0.0 159.4 jit_solution(6621733064520167486)
XLA Ops:
  0.0 2.8 %shard_map.64 = (bf16[1280,128]{1,0:T(8,128)(2,1)}, s32[2,128]{1,0:T(2,128)}) custom-call(s32[2,128]{1,0:T(2,128)} %bitcast.54, bf16[128,512]{1,0:T(8,128)(2,1)} %tokens_hbm.1), custom_call_target="tpu_custom_call" | custom-call | tf_op jit(solution)/shard_map/pallas_call | solution.py:191
  2.8 10.0 %all-to-all-start = ((bf16[16,80,128]{2,1,0:T(8,128)(2,1)}), bf16[16,80,128]{2,1,0:T(8,128)(2,1)S(1)}, u32[]{:S(2)}, u32[]{:S(2)}) async-start(bf16[16,80,128]{2,1,0:T(8,128)(2,1)} %bitcast.49), calls=%async_computation | async-start | bytes 655360 | tf_op jit(solution)/shard_map/all_to_all | solution.py:240
  13.5 12.3 %all-to-all-done = bf16[16,80,128]{2,1,0:T(8,128)(2,1)S(1)} async-done(((bf16[16,80,128]{2,1,0:T(8,128)(2,1)}), bf16[16,80,128]{2,1,0:T(8,128)(2,1)S(1)}, u32[]{:S(2)}, u32[]{:S(2)}) %all-to-all-start) | async-done | bytes 327712 | tf_op jit(solution)/shard_map/all_to_all | solution.py:240
  28.0 2.6 %collective-permute-start.1 = (bf16[2,640,128]{2,1,0:T(8,128)(2,1)S(1)}, bf16[2,640,128]{2,1,0:T(8,128)(2,1)S(1)}, u32[]{:S(2)}, u32[]{:S(2)}) collective-permute-start(bf16[2,640,128]{2,1,0:T(8,128)(2,1)S(1)} %pad_maximum_fusion.2), channel_id=1, source_target_pairs={{0,16},{1,5},{2,18},{3,7},{4,20},{5,1},{6,22},{7,3},{8,24},{9,13},... | collective-permute-start | bytes 983048 | tf_op jit(solution)/shard_map/ppermute | solution.py:286
  30.6 3.5 %collective-permute-done = bf16[2,640,128]{2,1,0:T(8,128)(2,1)S(1)} collective-permute-done((bf16[2,640,128]{2,1,0:T(8,128)(2,1)S(1)}, bf16[2,640,128]{2,1,0:T(8,128)(2,1)S(1)}, u32[]{:S(2)}, u32[]{:S(2)}) %collective-permute-start) | collective-permute-done | bytes 327712 | tf_op jit(solution)/shard_map/ppermute | solution.py:286
  35.7 2.9 %collective-permute-done.1 = bf16[2,640,128]{2,1,0:T(8,128)(2,1)S(1)} collective-permute-done((bf16[2,640,128]{2,1,0:T(8,128)(2,1)S(1)}, bf16[2,640,128]{2,1,0:T(8,128)(2,1)S(1)}, u32[]{:S(2)}, u32[]{:S(2)}) %collective-permute-start.1) | collective-permute-done | bytes 327712 | tf_op jit(solution)/shard_map/ppermute | solution.py:286
  38.6 1.7 %collective-permute-done.2 = bf16[2,640,128]{2,1,0:T(8,128)(2,1)S(1)} collective-permute-done((bf16[2,640,128]{2,1,0:T(8,128)(2,1)S(1)}, bf16[2,640,128]{2,1,0:T(8,128)(2,1)S(1)}, u32[]{:S(2)}, u32[]{:S(2)}) %collective-permute-start.2) | collective-permute-done | bytes 327712 | tf_op jit(solution)/shard_map/ppermute | solution.py:286
  41.4 2.9 %collective-permute-start.4 = (bf16[4,640,128]{2,1,0:T(8,128)(2,1)S(1)}, bf16[4,640,128]{2,1,0:T(8,128)(2,1)S(1)}, u32[]{:S(2)}, u32[]{:S(2)}) collective-permute-start(bf16[4,640,128]{2,1,0:T(8,128)(2,1)S(1)} %pad_maximum_fusion.g0), channel_id=1, source_target_pairs={{0,4},{1,17},{2,6},{3,19},{4,0},{5,21},{6,2},{7,23},{8,12},{9,25},... | collective-permute-start | bytes 1966088 | tf_op jit(solution)/shard_map/ppermute | solution.py:286
  44.3 7.2 %collective-permute-done.3.g1 = bf16[4,640,128]{2,1,0:T(8,128)(2,1)S(1)} collective-permute-done((bf16[4,640,128]{2,1,0:T(8,128)(2,1)S(1)}, bf16[4,640,128]{2,1,0:T(8,128)(2,1)S(1)}, u32[]{:S(2)}, u32[]{:S(2)}) %collective-permute-start.3) | collective-permute-done | bytes 655392 | tf_op jit(solution)/shard_map/ppermute | solution.py:286
  52.8 2.0 %copy-done = bf16[1,448,4096]{2,1,0:T(8,128)(2,1)S(1)} copy-done((bf16[1,448,4096]{2,1,0:T(8,128)(2,1)S(1)}, bf16[1,448,4096]{2,1,0:T(8,128)(2,1)}, u32[]{:S(2)}) %copy-start) | copy-done | bytes 3670040
  55.1 1.9 %copy-done.1 = bf16[448,4096]{1,0:T(8,128)(2,1)} copy-done((bf16[448,4096]{1,0:T(8,128)(2,1)}, bf16[448,4096]{1,0:T(8,128)(2,1)S(1)}, u32[]{:S(2)}) %copy-start.1) | copy-done | bytes 3670040
  57.2 2.4 %collective-permute-done.4.g2 = bf16[4,640,128]{2,1,0:T(8,128)(2,1)S(1)} collective-permute-done((bf16[4,640,128]{2,1,0:T(8,128)(2,1)S(1)}, bf16[4,640,128]{2,1,0:T(8,128)(2,1)S(1)}, u32[]{:S(2)}, u32[]{:S(2)}) %collective-permute-start.4) | collective-permute-done | bytes 655392 | tf_op jit(solution)/shard_map/ppermute | solution.py:286
  63.8 2.0 %copy-done.2 = bf16[448,4096]{1,0:T(8,128)(2,1)S(1)} copy-done((bf16[448,4096]{1,0:T(8,128)(2,1)S(1)}, bf16[448,4096]{1,0:T(8,128)(2,1)}, u32[]{:S(2)}) %copy-start.2) | copy-done | bytes 3670040
  65.8 12.0 %shard_map.66 = (bf16[4,640,128]{2,1,0:T(8,128)(2,1)S(1)}, bf16[4,640,128]{2,1,0:T(8,128)(2,1)S(1)}, bf16[4,640,128]{2,1,0:T(8,128)(2,1)S(1)}, bf16[4,640,128]{2,1,0:T(8,128)(2,1)S(1)}) custom-call(s32[2]{0:T(128)S(1)} %pad_add_fusion.where, bf16[4,640,128]{2,1,0:T(8,128)(2,1)S(1)} %pad_maximum_fusion.g0, ...), custom_call_target="tpu_custom_call" | custom-call | flops 7046430720 | bytes 31457280 | tf_op jit(solution)/shard_map/pallas_call | solution.py:112
  78.5 1.9 %collective-permute-start.11 = (bf16[4,640,128]{2,1,0:T(8,128)(2,1)S(1)}, bf16[4,640,128]{2,1,0:T(8,128)(2,1)S(1)}, u32[]{:S(2)}, u32[]{:S(2)}) collective-permute-start(bf16[4,640,128]{2,1,0:T(8,128)(2,1)S(1)} %get-tuple-element.19), channel_id=1, source_target_pairs={{0,4},{1,17},{2,6},{3,19},{4,0},{5,21},{6,2},{7,23},{8,12},{9,25},... | collective-permute-start | bytes 1966088 | tf_op jit(solution)/shard_map/ppermute | solution.py:286
  80.4 2.0 %collective-permute-start.9 = (bf16[4,640,128]{2,1,0:T(8,128)(2,1)S(1)}, bf16[4,640,128]{2,1,0:T(8,128)(2,1)S(1)}, u32[]{:S(2)}, u32[]{:S(2)}) collective-permute-start(bf16[4,640,128]{2,1,0:T(8,128)(2,1)S(1)} %get-tuple-element.17), channel_id=1, source_target_pairs={{0,6},{1,25},{2,0},{3,27},{4,2},{5,29},{6,4},{7,31},{8,14},{9,1},{... | collective-permute-start | bytes 1966088 | tf_op jit(solution)/shard_map/ppermute | solution.py:286
  82.3 11.8 %shard_map.67 = (bf16[4,640,128]{2,1,0:T(8,128)(2,1)S(1)}, bf16[4,640,128]{2,1,0:T(8,128)(2,1)S(1)}, bf16[4,640,128]{2,1,0:T(8,128)(2,1)S(1)}, bf16[4,640,128]{2,1,0:T(8,128)(2,1)S(1)}) custom-call(s32[2]{0:T(128)S(1)} %pad_add_fusion.where, bf16[4,640,128]{2,1,0:T(8,128)(2,1)S(1)} %pad_maximum_fusion.1.g0, ...), custom_call_target="tpu_custom_call" | custom-call | flops 7046430720 | bytes 31457280 | tf_op jit(solution)/shard_map/pallas_call | solution.py:112
  97.4 9.4 %collective-permute-start.12 = (bf16[640,128]{1,0:T(8,128)(2,1)S(1)}, bf16[640,128]{1,0:T(8,128)(2,1)S(1)}, u32[]{:S(2)}, u32[]{:S(2)}) collective-permute-start(bf16[640,128]{1,0:T(8,128)(2,1)S(1)} %get-tuple-element.25), channel_id=1, source_target_pairs={{0,24},{1,7},{2,26},{3,1},{4,28},{5,3},{6,30},{7,5},{8,0},{9,15},{... | collective-permute-start | bytes 491528 | tf_op jit(solution)/shard_map/ppermute | solution.py:286
  106.8 8.9 %collective-permute-start.14 = (bf16[640,128]{1,0:T(8,128)(2,1)S(1)}, bf16[640,128]{1,0:T(8,128)(2,1)S(1)}, u32[]{:S(2)}, u32[]{:S(2)}) collective-permute-start(bf16[640,128]{1,0:T(8,128)(2,1)S(1)} %get-tuple-element.26), channel_id=1, source_target_pairs={{0,16},{1,5},{2,18},{3,7},{4,20},{5,1},{6,22},{7,3},{8,24},{9,13},... | collective-permute-start | bytes 491528 | tf_op jit(solution)/shard_map/ppermute | solution.py:286
  116.1 7.7 %collective-permute-start.21 = (bf16[640,128]{1,0:T(8,128)(2,1)S(1)}, bf16[640,128]{1,0:T(8,128)(2,1)S(1)}, u32[]{:S(2)}, u32[]{:S(2)}) collective-permute-start(bf16[640,128]{1,0:T(8,128)(2,1)S(1)} %get-tuple-element.28), channel_id=1, source_target_pairs={{0,24},{1,7},{2,26},{3,1},{4,28},{5,3},{6,30},{7,5},{8,0},{9,15},{... | collective-permute-start | bytes 491528 | tf_op jit(solution)/shard_map/ppermute | solution.py:286
  124.4 3.7 %collective-permute-start.23 = (bf16[640,128]{1,0:T(8,128)(2,1)S(1)}, bf16[640,128]{1,0:T(8,128)(2,1)S(1)}, u32[]{:S(2)}, u32[]{:S(2)}) collective-permute-start(bf16[640,128]{1,0:T(8,128)(2,1)S(1)} %get-tuple-element.29), channel_id=1, source_target_pairs={{0,16},{1,5},{2,18},{3,7},{4,20},{5,1},{6,22},{7,3},{8,24},{9,13},... | collective-permute-start | bytes 491528 | tf_op jit(solution)/shard_map/ppermute | solution.py:286
  129.6 2.9 %collective-permute-done.23 = bf16[640,128]{1,0:T(8,128)(2,1)S(1)} collective-permute-done((bf16[640,128]{1,0:T(8,128)(2,1)S(1)}, bf16[640,128]{1,0:T(8,128)(2,1)S(1)}, u32[]{:S(2)}, u32[]{:S(2)}) %collective-permute-start.23) | collective-permute-done | bytes 163872 | tf_op jit(solution)/shard_map/ppermute | solution.py:286
  134.0 10.7 %all-to-all-start.1 = ((bf16[16,80,128]{2,1,0:T(8,128)(2,1)}), bf16[16,80,128]{2,1,0:T(8,128)(2,1)S(1)}, u32[]{:S(2)}, u32[]{:S(2)}) async-start(bf16[16,80,128]{2,1,0:T(8,128)(2,1)} %pad_maximum_fusion.3), calls=%async_computation.1 | async-start | bytes 655360 | tf_op jit(solution)/shard_map/all_to_all | solution.py:240
  145.4 12.5 %all-to-all-done.1 = bf16[16,80,128]{2,1,0:T(8,128)(2,1)S(1)} async-done(((bf16[16,80,128]{2,1,0:T(8,128)(2,1)}), bf16[16,80,128]{2,1,0:T(8,128)(2,1)S(1)}, u32[]{:S(2)}, u32[]{:S(2)}) %all-to-all-start.1) | async-done | bytes 327712 | tf_op jit(solution)/shard_map/all_to_all | solution.py:240
  (64 shorter events, 21.6 us)
Async XLA Ops:
  2.8 23.0 %all-to-all-start = ((bf16[16,80,128]{2,1,0:T(8,128)(2,1)}), bf16[16,80,128]{2,1,0:T(8,128)(2,1)S(1)}, u32[]{:S(2)}, u32[]{:S(2)}) async-start(bf16[16,80,128]{2,1,0:T(8,128)(2,1)} %bitcast.49), calls=%async_computation | async-start | bytes 655360 | tf_op jit(solution)/shard_map/all_to_all | solution.py:240
  12.7 49.6 %collective-permute-start.7 = (bf16[448,4096]{1,0:T(8,128)(2,1)}, bf16[448,4096]{1,0:T(8,128)(2,1)}, u32[]{:S(2)}, u32[]{:S(2)}) collective-permute-start(bf16[448,4096]{1,0:T(8,128)(2,1)} %bitcast.55), channel_id=1, source_target_pairs={{0,1},{1,0},{2,3},{3,2},{4,5},{5,4},{6,7},{7,6},{8,9},{9,8},{10,11... | collective-permute-start | bytes 11010056 | tf_op jit(solution)/shard_map/ppermute | solution.py:259
  12.9 50.8 %collective-permute-start.8 = (bf16[448,4096]{1,0:T(8,128)(2,1)}, bf16[448,4096]{1,0:T(8,128)(2,1)}, u32[]{:S(2)}, u32[]{:S(2)}) collective-permute-start(bf16[448,4096]{1,0:T(8,128)(2,1)} %bitcast.58), channel_id=1, source_target_pairs={{0,1},{1,0},{2,3},{3,2},{4,5},{5,4},{6,7},{7,6},{8,9},{9,8},{10,11... | collective-permute-start | bytes 11010056 | tf_op jit(solution)/shard_map/ppermute | solution.py:259
  13.3 50.5 %collective-permute-start.6 = (bf16[448,4096]{1,0:T(8,128)(2,1)}, bf16[448,4096]{1,0:T(8,128)(2,1)}, u32[]{:S(2)}, u32[]{:S(2)}) collective-permute-start(bf16[448,4096]{1,0:T(8,128)(2,1)} %bitcast.44), channel_id=1, source_target_pairs={{0,1},{1,0},{2,3},{3,2},{4,5},{5,4},{6,7},{7,6},{8,9},{9,8},{10,11... | collective-permute-start | bytes 11010056 | tf_op jit(solution)/shard_map/ppermute | solution.py:259
  26.6 7.5 %collective-permute-start = (bf16[2,640,128]{2,1,0:T(8,128)(2,1)S(1)}, bf16[2,640,128]{2,1,0:T(8,128)(2,1)S(1)}, u32[]{:S(2)}, u32[]{:S(2)}) collective-permute-start(bf16[2,640,128]{2,1,0:T(8,128)(2,1)S(1)} %pad_maximum_fusion.2), channel_id=1, source_target_pairs={{0,8},{1,3},{2,10},{3,5},{4,12},{5,7},{6,14},{7,1},{8,16},{9,11},{... | collective-permute-start | bytes 983048 | tf_op jit(solution)/shard_map/ppermute | solution.py:286
  28.0 10.6 %collective-permute-start.1 = (bf16[2,640,128]{2,1,0:T(8,128)(2,1)S(1)}, bf16[2,640,128]{2,1,0:T(8,128)(2,1)S(1)}, u32[]{:S(2)}, u32[]{:S(2)}) collective-permute-start(bf16[2,640,128]{2,1,0:T(8,128)(2,1)S(1)} %pad_maximum_fusion.2), channel_id=1, source_target_pairs={{0,16},{1,5},{2,18},{3,7},{4,20},{5,1},{6,22},{7,3},{8,24},{9,13},... | collective-permute-start | bytes 983048 | tf_op jit(solution)/shard_map/ppermute | solution.py:286
  40.4 11.0 %collective-permute-start.3 = (bf16[4,640,128]{2,1,0:T(8,128)(2,1)S(1)}, bf16[4,640,128]{2,1,0:T(8,128)(2,1)S(1)}, u32[]{:S(2)}, u32[]{:S(2)}) collective-permute-start(bf16[4,640,128]{2,1,0:T(8,128)(2,1)S(1)} %pad_maximum_fusion.g0), channel_id=1, source_target_pairs={{0,2},{1,9},{2,4},{3,11},{4,6},{5,13},{6,0},{7,15},{8,10},{9,17},{... | collective-permute-start | bytes 1966088 | tf_op jit(solution)/shard_map/ppermute | solution.py:286
  41.4 18.2 %collective-permute-start.4 = (bf16[4,640,128]{2,1,0:T(8,128)(2,1)S(1)}, bf16[4,640,128]{2,1,0:T(8,128)(2,1)S(1)}, u32[]{:S(2)}, u32[]{:S(2)}) collective-permute-start(bf16[4,640,128]{2,1,0:T(8,128)(2,1)S(1)} %pad_maximum_fusion.g0), channel_id=1, source_target_pairs={{0,4},{1,17},{2,6},{3,19},{4,0},{5,21},{6,2},{7,23},{8,12},{9,25},... | collective-permute-start | bytes 1966088 | tf_op jit(solution)/shard_map/ppermute | solution.py:286
  51.5 9.7 %collective-permute-start.5 = (bf16[4,640,128]{2,1,0:T(8,128)(2,1)S(1)}, bf16[4,640,128]{2,1,0:T(8,128)(2,1)S(1)}, u32[]{:S(2)}, u32[]{:S(2)}) collective-permute-start(bf16[4,640,128]{2,1,0:T(8,128)(2,1)S(1)} %pad_maximum_fusion.g0), channel_id=1, source_target_pairs={{0,6},{1,25},{2,0},{3,27},{4,2},{5,29},{6,4},{7,31},{8,14},{9,1},{... | collective-permute-start | bytes 1966088 | tf_op jit(solution)/shard_map/ppermute | solution.py:286
  59.6 20.8 %collective-permute-start.15 = (bf16[4,640,128]{2,1,0:T(8,128)(2,1)S(1)}, bf16[4,640,128]{2,1,0:T(8,128)(2,1)S(1)}, u32[]{:S(2)}, u32[]{:S(2)}) collective-permute-start(bf16[4,640,128]{2,1,0:T(8,128)(2,1)S(1)} %pad_maximum_fusion.1.g0), channel_id=1, source_target_pairs={{0,2},{1,9},{2,4},{3,11},{4,6},{5,13},{6,0},{7,15},{8,10},{9,17},{... | collective-permute-start | bytes 1966088 | tf_op jit(solution)/shard_map/ppermute | solution.py:286
  61.2 21.1 %collective-permute-start.16 = (bf16[4,640,128]{2,1,0:T(8,128)(2,1)S(1)}, bf16[4,640,128]{2,1,0:T(8,128)(2,1)S(1)}, u32[]{:S(2)}, u32[]{:S(2)}) collective-permute-start(bf16[4,640,128]{2,1,0:T(8,128)(2,1)S(1)} %pad_maximum_fusion.1.g0), channel_id=1, source_target_pairs={{0,4},{1,17},{2,6},{3,19},{4,0},{5,21},{6,2},{7,23},{8,12},{9,25},... | collective-permute-start | bytes 1966088 | tf_op jit(solution)/shard_map/ppermute | solution.py:286
  62.4 19.9 %collective-permute-start.17 = (bf16[4,640,128]{2,1,0:T(8,128)(2,1)S(1)}, bf16[4,640,128]{2,1,0:T(8,128)(2,1)S(1)}, u32[]{:S(2)}, u32[]{:S(2)}) collective-permute-start(bf16[4,640,128]{2,1,0:T(8,128)(2,1)S(1)} %pad_maximum_fusion.1.g0), channel_id=1, source_target_pairs={{0,6},{1,25},{2,0},{3,27},{4,2},{5,29},{6,4},{7,31},{8,14},{9,1},{... | collective-permute-start | bytes 1966088 | tf_op jit(solution)/shard_map/ppermute | solution.py:286
  77.8 18.0 %collective-permute-start.10 = (bf16[4,640,128]{2,1,0:T(8,128)(2,1)S(1)}, bf16[4,640,128]{2,1,0:T(8,128)(2,1)S(1)}, u32[]{:S(2)}, u32[]{:S(2)}) collective-permute-start(bf16[4,640,128]{2,1,0:T(8,128)(2,1)S(1)} %get-tuple-element.18), channel_id=1, source_target_pairs={{0,2},{1,9},{2,4},{3,11},{4,6},{5,13},{6,0},{7,15},{8,10},{9,17},{... | collective-permute-start | bytes 1966088 | tf_op jit(solution)/shard_map/ppermute | solution.py:286
  78.5 18.5 %collective-permute-start.11 = (bf16[4,640,128]{2,1,0:T(8,128)(2,1)S(1)}, bf16[4,640,128]{2,1,0:T(8,128)(2,1)S(1)}, u32[]{:S(2)}, u32[]{:S(2)}) collective-permute-start(bf16[4,640,128]{2,1,0:T(8,128)(2,1)S(1)} %get-tuple-element.19), channel_id=1, source_target_pairs={{0,4},{1,17},{2,6},{3,19},{4,0},{5,21},{6,2},{7,23},{8,12},{9,25},... | collective-permute-start | bytes 1966088 | tf_op jit(solution)/shard_map/ppermute | solution.py:286
  80.4 16.7 %collective-permute-start.9 = (bf16[4,640,128]{2,1,0:T(8,128)(2,1)S(1)}, bf16[4,640,128]{2,1,0:T(8,128)(2,1)S(1)}, u32[]{:S(2)}, u32[]{:S(2)}) collective-permute-start(bf16[4,640,128]{2,1,0:T(8,128)(2,1)S(1)} %get-tuple-element.17), channel_id=1, source_target_pairs={{0,6},{1,25},{2,0},{3,27},{4,2},{5,29},{6,4},{7,31},{8,14},{9,1},{... | collective-permute-start | bytes 1966088 | tf_op jit(solution)/shard_map/ppermute | solution.py:286
  94.2 12.7 %collective-permute-start.18 = (bf16[4,640,128]{2,1,0:T(8,128)(2,1)S(1)}, bf16[4,640,128]{2,1,0:T(8,128)(2,1)S(1)}, u32[]{:S(2)}, u32[]{:S(2)}) collective-permute-start(bf16[4,640,128]{2,1,0:T(8,128)(2,1)S(1)} %get-tuple-element.21), channel_id=1, source_target_pairs={{0,6},{1,25},{2,0},{3,27},{4,2},{5,29},{6,4},{7,31},{8,14},{9,1},{... | collective-permute-start | bytes 1966088 | tf_op jit(solution)/shard_map/ppermute | solution.py:286
  94.3 21.4 %collective-permute-start.19 = (bf16[4,640,128]{2,1,0:T(8,128)(2,1)S(1)}, bf16[4,640,128]{2,1,0:T(8,128)(2,1)S(1)}, u32[]{:S(2)}, u32[]{:S(2)}) collective-permute-start(bf16[4,640,128]{2,1,0:T(8,128)(2,1)S(1)} %get-tuple-element.22), channel_id=1, source_target_pairs={{0,2},{1,9},{2,4},{3,11},{4,6},{5,13},{6,0},{7,15},{8,10},{9,17},{... | collective-permute-start | bytes 1966088 | tf_op jit(solution)/shard_map/ppermute | solution.py:286
  95.8 19.8 %collective-permute-start.20 = (bf16[4,640,128]{2,1,0:T(8,128)(2,1)S(1)}, bf16[4,640,128]{2,1,0:T(8,128)(2,1)S(1)}, u32[]{:S(2)}, u32[]{:S(2)}) collective-permute-start(bf16[4,640,128]{2,1,0:T(8,128)(2,1)S(1)} %get-tuple-element.23), channel_id=1, source_target_pairs={{0,4},{1,17},{2,6},{3,19},{4,0},{5,21},{6,2},{7,23},{8,12},{9,25},... | collective-permute-start | bytes 1966088 | tf_op jit(solution)/shard_map/ppermute | solution.py:286
  97.4 27.0 %collective-permute-start.12 = (bf16[640,128]{1,0:T(8,128)(2,1)S(1)}, bf16[640,128]{1,0:T(8,128)(2,1)S(1)}, u32[]{:S(2)}, u32[]{:S(2)}) collective-permute-start(bf16[640,128]{1,0:T(8,128)(2,1)S(1)} %get-tuple-element.25), channel_id=1, source_target_pairs={{0,24},{1,7},{2,26},{3,1},{4,28},{5,3},{6,30},{7,5},{8,0},{9,15},{... | collective-permute-start | bytes 491528 | tf_op jit(solution)/shard_map/ppermute | solution.py:286
  106.8 21.3 %collective-permute-start.13 = (bf16[640,128]{1,0:T(8,128)(2,1)S(1)}, bf16[640,128]{1,0:T(8,128)(2,1)S(1)}, u32[]{:S(2)}, u32[]{:S(2)}) collective-permute-start(bf16[640,128]{1,0:T(8,128)(2,1)S(1)} %get-tuple-element.27), channel_id=1, source_target_pairs={{0,8},{1,3},{2,10},{3,5},{4,12},{5,7},{6,14},{7,1},{8,16},{9,11},{... | collective-permute-start | bytes 491528 | tf_op jit(solution)/shard_map/ppermute | solution.py:286
  106.8 21.3 %collective-permute-start.14 = (bf16[640,128]{1,0:T(8,128)(2,1)S(1)}, bf16[640,128]{1,0:T(8,128)(2,1)S(1)}, u32[]{:S(2)}, u32[]{:S(2)}) collective-permute-start(bf16[640,128]{1,0:T(8,128)(2,1)S(1)} %get-tuple-element.26), channel_id=1, source_target_pairs={{0,16},{1,5},{2,18},{3,7},{4,20},{5,1},{6,22},{7,3},{8,24},{9,13},... | collective-permute-start | bytes 491528 | tf_op jit(solution)/shard_map/ppermute | solution.py:286
  116.1 12.7 %collective-permute-start.21 = (bf16[640,128]{1,0:T(8,128)(2,1)S(1)}, bf16[640,128]{1,0:T(8,128)(2,1)S(1)}, u32[]{:S(2)}, u32[]{:S(2)}) collective-permute-start(bf16[640,128]{1,0:T(8,128)(2,1)S(1)} %get-tuple-element.28), channel_id=1, source_target_pairs={{0,24},{1,7},{2,26},{3,1},{4,28},{5,3},{6,30},{7,5},{8,0},{9,15},{... | collective-permute-start | bytes 491528 | tf_op jit(solution)/shard_map/ppermute | solution.py:286
  124.4 8.2 %collective-permute-start.23 = (bf16[640,128]{1,0:T(8,128)(2,1)S(1)}, bf16[640,128]{1,0:T(8,128)(2,1)S(1)}, u32[]{:S(2)}, u32[]{:S(2)}) collective-permute-start(bf16[640,128]{1,0:T(8,128)(2,1)S(1)} %get-tuple-element.29), channel_id=1, source_target_pairs={{0,16},{1,5},{2,18},{3,7},{4,20},{5,1},{6,22},{7,3},{8,24},{9,13},... | collective-permute-start | bytes 491528 | tf_op jit(solution)/shard_map/ppermute | solution.py:286
  134.0 23.9 %all-to-all-start.1 = ((bf16[16,80,128]{2,1,0:T(8,128)(2,1)}), bf16[16,80,128]{2,1,0:T(8,128)(2,1)S(1)}, u32[]{:S(2)}, u32[]{:S(2)}) async-start(bf16[16,80,128]{2,1,0:T(8,128)(2,1)} %pad_maximum_fusion.3), calls=%async_computation.1 | async-start | bytes 655360 | tf_op jit(solution)/shard_map/all_to_all | solution.py:240
  (7 other events, 45.3 us)
